TPU v7x, 32 devices: a whole 2x2x4 slice. The times are simulated.
32 devices in a mesh: dp: 2 (over x), pp: 4 (over z), sp: 4 (over y, core).
Axes of the slice: x: 2, y: 2, z: 4, core: 2. Of those that a mesh axis runs over, the one named last changes fastest.
Arguments:
- latent_in: float32 [4, 512, 16], P('dp', 'sp'), parts along dimension 0
- pos_embed: bfloat16 [2, 512, 1152], P(None, 'sp')
- condition: bfloat16 [4, 1152], P('dp'), parts along dimension 0
- step_size: float32 [4], P('dp'), parts along dimension 0
- w_in: bfloat16 [16, 1152], replicated
- w_ada: bfloat16 [8, 1152, 6912], replicated
- w_qkv: bfloat16 [8, 1152, 3456], replicated
- w_o: bfloat16 [8, 1152, 1152], replicated
- w_up: bfloat16 [8, 1152, 4608], replicated
- w_down: bfloat16 [8, 4608, 1152], replicated
- b_layer: bfloat16 [8, 17280], replicated
- w_fa: bfloat16 [1152, 2304], replicated
- b_fa: bfloat16 [2304], replicated
- w_out: bfloat16 [1152, 16], replicated
- k_old: bfloat16 [16, 1024, 16, 72], P('dp'), parts along dimension 0
- v_old: bfloat16 [16, 1024, 16, 72], P('dp'), parts along dimension 0
Outputs:
- output: float32 [4, 512, 16], P('dp', 'sp'), parts along dimension 0
There are 2 independent parts. A program takes and returns all parts, laid end to end along the dimension named above; an argument that names none is the same for every part.
All inputs are finite; a program needn't handle non-finite values.
Results may differ from a plain program's by a relative error of at most 0.0134576.
Values are sent between devices in bfloat16 or wider.
A program may use at most 1.75 GiB of HBM per device.

v0:
```python
import jax
import jax.numpy as jnp
from jax import lax
from jax.sharding import PartitionSpec as P

LN_EPS = 1e-6


def layer_norm(hidden):
    mean_val = jnp.mean(hidden, axis=-1, keepdims=True)
    centered = hidden - mean_val
    var_val = jnp.mean(centered * centered, axis=-1, keepdims=True)
    return centered * lax.rsqrt(var_val + LN_EPS)


def solution(mesh):
    num_stages = mesh.shape["pp"]
    split_count = mesh.shape["sp"]
    forward_perm = [(src_stage, src_stage + 1) for src_stage in range(num_stages - 1)]
    return_perm = [(num_stages - 1, 0)]
    row_spec = P("dp", "sp", None)
    full_spec = P()
    buf_spec = P("dp", None, None, None)
    in_specs = (row_spec, P(None, "sp", None), P("dp", None), P("dp"), full_spec, full_spec, full_spec, full_spec, full_spec, full_spec, full_spec, full_spec, full_spec, full_spec, buf_spec, buf_spec)

    def device_fn(latent_in, pos_embed, condition, step_size, w_in, w_ada, w_qkv, w_o, w_up, w_down, b_layer, w_fa, b_fa, w_out, k_old, v_old):
        num_patches = latent_in.shape[0]
        sub_rows = latent_in.shape[1]
        patch_rows = sub_rows * split_count
        model_width = w_in.shape[1]
        stage_layers = w_qkv.shape[0] // num_stages
        num_heads = k_old.shape[2]
        head_dim = k_old.shape[3]
        attn_scale = head_dim ** -0.5
        stage_idx = lax.axis_index("pp")
        is_last = stage_idx == num_stages - 1
        first_layer = stage_idx * stage_layers
        ada_stage = lax.dynamic_slice_in_dim(w_ada, first_layer, stage_layers, axis=0)
        qkv_stage = lax.dynamic_slice_in_dim(w_qkv, first_layer, stage_layers, axis=0)
        out_stage = lax.dynamic_slice_in_dim(w_o, first_layer, stage_layers, axis=0)
        up_stage = lax.dynamic_slice_in_dim(w_up, first_layer, stage_layers, axis=0)
        down_stage = lax.dynamic_slice_in_dim(w_down, first_layer, stage_layers, axis=0)
        bias_stage = lax.dynamic_slice_in_dim(b_layer, first_layer, stage_layers, axis=0).astype(jnp.float32)
        b_fa32 = b_fa.astype(jnp.float32)
        key_bufs = [lax.dynamic_index_in_dim(k_old, first_layer + layer_j, axis=0, keepdims=False) for layer_j in range(stage_layers)]
        value_bufs = [lax.dynamic_index_in_dim(v_old, first_layer + layer_j, axis=0, keepdims=False) for layer_j in range(stage_layers)]

        def run_layer(hidden, mod_vec, layer_j, key_buf, value_buf, row_start, is_valid):
            bias_row = bias_stage[layer_j]
            scale_attn, shift_attn, gate_attn, scale_mlp, shift_mlp, gate_mlp = jnp.split(mod_vec, 6)
            normed = (layer_norm(hidden.astype(jnp.float32)) * (1.0 + scale_attn) + shift_attn).astype(jnp.bfloat16)
            qkv_rows = (jnp.dot(normed, qkv_stage[layer_j], preferred_element_type=jnp.float32) + bias_row[6 * model_width:9 * model_width]).astype(jnp.bfloat16)
            kv_patch = lax.all_gather(qkv_rows[:, model_width:], "sp", axis=0, tiled=True)
            key_new = kv_patch[:, :model_width].reshape(patch_rows, num_heads, head_dim)
            value_new = kv_patch[:, model_width:].reshape(patch_rows, num_heads, head_dim)
            key_prev = lax.dynamic_slice_in_dim(key_buf, row_start, patch_rows, axis=0)
            value_prev = lax.dynamic_slice_in_dim(value_buf, row_start, patch_rows, axis=0)
            key_buf = lax.dynamic_update_slice_in_dim(key_buf, jnp.where(is_valid, key_new, key_prev), row_start, axis=0)
            value_buf = lax.dynamic_update_slice_in_dim(value_buf, jnp.where(is_valid, value_new, value_prev), row_start, axis=0)
            query_rows = qkv_rows[:, :model_width].reshape(sub_rows, num_heads, head_dim)
            logits = jnp.einsum("rhd,nhd->hrn", query_rows, key_buf, preferred_element_type=jnp.float32) * attn_scale
            attn_prob = jax.nn.softmax(logits, axis=-1).astype(jnp.bfloat16)
            attn_rows = jnp.einsum("hrn,nhd->rhd", attn_prob, value_buf, preferred_element_type=jnp.float32).astype(jnp.bfloat16).reshape(sub_rows, model_width)
            residual = hidden.astype(jnp.float32) + gate_attn * (jnp.dot(attn_rows, out_stage[layer_j], preferred_element_type=jnp.float32) + bias_row[9 * model_width:10 * model_width])
            mlp_in = (layer_norm(residual) * (1.0 + scale_mlp) + shift_mlp).astype(jnp.bfloat16)
            mlp_mid = jax.nn.gelu(jnp.dot(mlp_in, up_stage[layer_j], preferred_element_type=jnp.float32) + bias_row[10 * model_width:14 * model_width], approximate=True).astype(jnp.bfloat16)
            hidden = (residual + gate_mlp * (jnp.dot(mlp_mid, down_stage[layer_j], preferred_element_type=jnp.float32) + bias_row[14 * model_width:])).astype(jnp.bfloat16)
            return hidden, key_buf, value_buf

        def run_step(step_idx, x_source, latent_cur, keys_start, values_start):
            cond_act = jax.nn.silu(condition[step_idx].astype(jnp.float32)).astype(jnp.bfloat16)
            mod_stage = jnp.einsum("c,lcf->lf", cond_act, ada_stage, preferred_element_type=jnp.float32) + bias_stage[:, :6 * model_width]
            final_mod = jnp.dot(cond_act[None, :], w_fa, preferred_element_type=jnp.float32)[0] + b_fa32
            scale_out, shift_out = jnp.split(final_mod, 2)
            step_val = step_size[step_idx]

            def tick_body(tick_idx, loop_state):
                received, latent_acc, keys_in, values_in = loop_state
                patch_idx = tick_idx - stage_idx
                is_valid = (patch_idx >= 0) & (patch_idx < num_patches)
                patch_safe = jnp.clip(patch_idx, 0, num_patches - 1)
                row_start = patch_safe * patch_rows
                x_rows = lax.dynamic_index_in_dim(x_source, patch_safe, axis=0, keepdims=False)
                pos_rows = lax.dynamic_index_in_dim(pos_embed, patch_safe, axis=0, keepdims=False)
                embedded = (jnp.dot(x_rows, w_in, preferred_element_type=jnp.float32) + pos_rows.astype(jnp.float32)).astype(jnp.bfloat16)
                hidden = jnp.where(stage_idx == 0, embedded, received)
                keys_out = []
                values_out = []
                for layer_j in range(stage_layers):
                    hidden, key_buf, value_buf = run_layer(hidden, mod_stage[layer_j], layer_j, keys_in[layer_j], values_in[layer_j], row_start, is_valid)
                    keys_out.append(key_buf)
                    values_out.append(value_buf)
                out_in = (layer_norm(hidden.astype(jnp.float32)) * (1.0 + scale_out) + shift_out).astype(jnp.bfloat16)
                velocity = jnp.dot(out_in, w_out, preferred_element_type=jnp.float32)
                x_old = lax.dynamic_index_in_dim(latent_acc, patch_safe, axis=0, keepdims=False)
                x_new = jnp.where(is_valid & is_last, x_old + step_val * velocity, x_old)
                latent_acc = lax.dynamic_update_index_in_dim(latent_acc, x_new, patch_safe, axis=0)
                sent_rows = lax.ppermute(hidden, "pp", forward_perm)
                return (sent_rows, latent_acc, keys_out, values_out)

            start_state = (jnp.zeros((sub_rows, model_width), jnp.bfloat16), latent_cur, keys_start, values_start)
            end_state = lax.fori_loop(0, num_patches + num_stages - 1, tick_body, start_state)
            return end_state[1], end_state[2], end_state[3]

        latent_cur, key_bufs, value_bufs = run_step(0, latent_in.astype(jnp.bfloat16), latent_in, key_bufs, value_bufs)
        x_source = lax.ppermute(latent_cur.astype(jnp.bfloat16), "pp", return_perm)
        latent_cur, key_bufs, value_bufs = run_step(1, x_source, latent_cur, key_bufs, value_bufs)
        return lax.psum(jnp.where(is_last, latent_cur, 0.0), "pp")

    return jax.shard_map(device_fn, mesh=mesh, in_specs=in_specs, out_specs=row_spec, check_vma=False)
```

profile of v0, /device:TPU:0, one launch (start us, length us, event | category | flops | bytes accessed | tf_op | source)
XLA Modules:
  0.0 1552.0 jit_solution(7300565695234391230)
XLA Ops:
  73.4 17.4 %constant_dynamic-slice_fusion.2 = bf16[2,4608,1152]{2,1,0:T(8,128)(2,1)} fusion(bf16[8,4608,1152]{2,1,0:T(8,128)(2,1)} %param.29, s32[]{:T(128)S(6)} %select_n.226), kind=kLoop, calls=%fused_computation.383 | loop fusion | bytes 42467332 | tf_op jit(solution)/shard_map/dynamic_slice | solution.py:42
  101.4 703.4 %while.48 = (s32[]{:T(128)}, bf16[128,1152]{1,0:T(8,128)(2,1)S(1)}, f32[2,128,16]{1,2,0:T(8,128)S(1)}, bf16[1024,16,72]{0,2,1:T(8,128)(2,1)}, bf16[1024,16,72]{0...) while((s32[]{:T(128)}, bf16[128,1152]{1,0:T(8,128)(2,1)S(1)}, ...), condition=%wide.region_15.16_spmd, body=%wide.region_0.15_spmd.sunk | while | flops 9418356736 | bytes 249631504 | solution.py:102
  112.2 25.0 %all-gather.5.cloned.1.call-done = bf16[512,2304]{1,0:T(8,128)(2,1)} async-done(((bf16[128,2304]{1,0:T(8,128)(2,1)}), bf16[512,2304]{1,0:T(8,128)(2,1)}) %all-gather.5.cloned.1.call-update) | async-done | bytes 2359312 | tf_op jit(solution)/shard_map/while/body/eval_jaxpr/all_gather | solution.py:53
  181.3 21.7 %all-gather.7.cloned.1.call-done = bf16[512,2304]{1,0:T(8,128)(2,1)} async-done(((bf16[128,2304]{1,0:T(8,128)(2,1)}), bf16[512,2304]{1,0:T(8,128)(2,1)}) %all-gather.7.cloned.1.call-update) | async-done | bytes 2359312 | tf_op jit(solution)/shard_map/while/body/eval_jaxpr/all_gather | solution.py:53
  254.2 23.3 %all-gather.5.cloned.1.call-done = bf16[512,2304]{1,0:T(8,128)(2,1)} async-done(((bf16[128,2304]{1,0:T(8,128)(2,1)}), bf16[512,2304]{1,0:T(8,128)(2,1)}) %all-gather.5.cloned.1.call-update) | async-done | bytes 2359312 | tf_op jit(solution)/shard_map/while/body/eval_jaxpr/all_gather | solution.py:53
  321.6 21.7 %all-gather.7.cloned.1.call-done = bf16[512,2304]{1,0:T(8,128)(2,1)} async-done(((bf16[128,2304]{1,0:T(8,128)(2,1)}), bf16[512,2304]{1,0:T(8,128)(2,1)}) %all-gather.7.cloned.1.call-update) | async-done | bytes 2359312 | tf_op jit(solution)/shard_map/while/body/eval_jaxpr/all_gather | solution.py:53
  394.5 23.3 %all-gather.5.cloned.1.call-done = bf16[512,2304]{1,0:T(8,128)(2,1)} async-done(((bf16[128,2304]{1,0:T(8,128)(2,1)}), bf16[512,2304]{1,0:T(8,128)(2,1)}) %all-gather.5.cloned.1.call-update) | async-done | bytes 2359312 | tf_op jit(solution)/shard_map/while/body/eval_jaxpr/all_gather | solution.py:53
  461.8 21.7 %all-gather.7.cloned.1.call-done = bf16[512,2304]{1,0:T(8,128)(2,1)} async-done(((bf16[128,2304]{1,0:T(8,128)(2,1)}), bf16[512,2304]{1,0:T(8,128)(2,1)}) %all-gather.7.cloned.1.call-update) | async-done | bytes 2359312 | tf_op jit(solution)/shard_map/while/body/eval_jaxpr/all_gather | solution.py:53
  534.8 23.2 %all-gather.5.cloned.1.call-done = bf16[512,2304]{1,0:T(8,128)(2,1)} async-done(((bf16[128,2304]{1,0:T(8,128)(2,1)}), bf16[512,2304]{1,0:T(8,128)(2,1)}) %all-gather.5.cloned.1.call-update) | async-done | bytes 2359312 | tf_op jit(solution)/shard_map/while/body/eval_jaxpr/all_gather | solution.py:53
  602.1 21.7 %all-gather.7.cloned.1.call-done = bf16[512,2304]{1,0:T(8,128)(2,1)} async-done(((bf16[128,2304]{1,0:T(8,128)(2,1)}), bf16[512,2304]{1,0:T(8,128)(2,1)}) %all-gather.7.cloned.1.call-update) | async-done | bytes 2359312 | tf_op jit(solution)/shard_map/while/body/eval_jaxpr/all_gather | solution.py:53
  675.1 23.2 %all-gather.5.cloned.1.call-done = bf16[512,2304]{1,0:T(8,128)(2,1)} async-done(((bf16[128,2304]{1,0:T(8,128)(2,1)}), bf16[512,2304]{1,0:T(8,128)(2,1)}) %all-gather.5.cloned.1.call-update) | async-done | bytes 2359312 | tf_op jit(solution)/shard_map/while/body/eval_jaxpr/all_gather | solution.py:53
  742.4 21.7 %all-gather.7.cloned.1.call-done = bf16[512,2304]{1,0:T(8,128)(2,1)} async-done(((bf16[128,2304]{1,0:T(8,128)(2,1)}), bf16[512,2304]{1,0:T(8,128)(2,1)}) %all-gather.7.cloned.1.call-update) | async-done | bytes 2359312 | tf_op jit(solution)/shard_map/while/body/eval_jaxpr/all_gather | solution.py:53
  812.2 712.4 %while.49 = (s32[]{:T(128)}, bf16[128,1152]{1,0:T(8,128)(2,1)S(1)}, f32[2,128,16]{1,2,0:T(8,128)S(1)}, bf16[1024,16,72]{0,2,1:T(8,128)(2,1)}, bf16[1024,16,72]{0...) while((s32[]{:T(128)}, bf16[128,1152]{1,0:T(8,128)(2,1)S(1)}, ...), condition=%wide.region_31.32_spmd, body=%wide.region_16.31_spmd.sunk | while | flops 9418356736 | bytes 249631504 | solution.py:102
  837.6 19.5 %all-gather.9.cloned.1.call-done = bf16[512,2304]{1,0:T(8,128)(2,1)} async-done(((bf16[128,2304]{1,0:T(8,128)(2,1)}), bf16[512,2304]{1,0:T(8,128)(2,1)}) %all-gather.9.cloned.1.call-update) | async-done | bytes 2359312 | tf_op jit(solution)/shard_map/while/body/eval_jaxpr/all_gather | solution.py:53
  901.1 21.7 %all-gather.11.cloned.1.call-done = bf16[512,2304]{1,0:T(8,128)(2,1)} async-done(((bf16[128,2304]{1,0:T(8,128)(2,1)}), bf16[512,2304]{1,0:T(8,128)(2,1)}) %all-gather.11.cloned.1.call-update) | async-done | bytes 2359312 | tf_op jit(solution)/shard_map/while/body/eval_jaxpr/all_gather | solution.py:53
  974.0 23.3 %all-gather.9.cloned.1.call-done = bf16[512,2304]{1,0:T(8,128)(2,1)} async-done(((bf16[128,2304]{1,0:T(8,128)(2,1)}), bf16[512,2304]{1,0:T(8,128)(2,1)}) %all-gather.9.cloned.1.call-update) | async-done | bytes 2359312 | tf_op jit(solution)/shard_map/while/body/eval_jaxpr/all_gather | solution.py:53
  1041.4 21.7 %all-gather.11.cloned.1.call-done = bf16[512,2304]{1,0:T(8,128)(2,1)} async-done(((bf16[128,2304]{1,0:T(8,128)(2,1)}), bf16[512,2304]{1,0:T(8,128)(2,1)}) %all-gather.11.cloned.1.call-update) | async-done | bytes 2359312 | tf_op jit(solution)/shard_map/while/body/eval_jaxpr/all_gather | solution.py:53
  1114.3 23.3 %all-gather.9.cloned.1.call-done = bf16[512,2304]{1,0:T(8,128)(2,1)} async-done(((bf16[128,2304]{1,0:T(8,128)(2,1)}), bf16[512,2304]{1,0:T(8,128)(2,1)}) %all-gather.9.cloned.1.call-update) | async-done | bytes 2359312 | tf_op jit(solution)/shard_map/while/body/eval_jaxpr/all_gather | solution.py:53
  1181.6 21.7 %all-gather.11.cloned.1.call-done = bf16[512,2304]{1,0:T(8,128)(2,1)} async-done(((bf16[128,2304]{1,0:T(8,128)(2,1)}), bf16[512,2304]{1,0:T(8,128)(2,1)}) %all-gather.11.cloned.1.call-update) | async-done | bytes 2359312 | tf_op jit(solution)/shard_map/while/body/eval_jaxpr/all_gather | solution.py:53
  1254.6 23.2 %all-gather.9.cloned.1.call-done = bf16[512,2304]{1,0:T(8,128)(2,1)} async-done(((bf16[128,2304]{1,0:T(8,128)(2,1)}), bf16[512,2304]{1,0:T(8,128)(2,1)}) %all-gather.9.cloned.1.call-update) | async-done | bytes 2359312 | tf_op jit(solution)/shard_map/while/body/eval_jaxpr/all_gather | solution.py:53
  1321.9 21.7 %all-gather.11.cloned.1.call-done = bf16[512,2304]{1,0:T(8,128)(2,1)} async-done(((bf16[128,2304]{1,0:T(8,128)(2,1)}), bf16[512,2304]{1,0:T(8,128)(2,1)}) %all-gather.11.cloned.1.call-update) | async-done | bytes 2359312 | tf_op jit(solution)/shard_map/while/body/eval_jaxpr/all_gather | solution.py:53
  1394.9 23.2 %all-gather.9.cloned.1.call-done = bf16[512,2304]{1,0:T(8,128)(2,1)} async-done(((bf16[128,2304]{1,0:T(8,128)(2,1)}), bf16[512,2304]{1,0:T(8,128)(2,1)}) %all-gather.9.cloned.1.call-update) | async-done | bytes 2359312 | tf_op jit(solution)/shard_map/while/body/eval_jaxpr/all_gather | solution.py:53
  1462.2 21.7 %all-gather.11.cloned.1.call-done = bf16[512,2304]{1,0:T(8,128)(2,1)} async-done(((bf16[128,2304]{1,0:T(8,128)(2,1)}), bf16[512,2304]{1,0:T(8,128)(2,1)}) %all-gather.11.cloned.1.call-update) | async-done | bytes 2359312 | tf_op jit(solution)/shard_map/while/body/eval_jaxpr/all_gather | solution.py:53
  1524.6 20.4 %psum.7 = f32[2,128,16]{1,2,0:T(8,128)} all-reduce(f32[2,128,16]{1,2,0:T(8,128)S(1)} %broadcast_select_fusion), channel_id=1, replica_groups=mesh['dp'=2,'pp'=4,'sp'=4] {'pp'}, use_global_device_ids=true, to_apply=%region_32.33 | all-reduce | flops 4096 | bytes 32768 | tf_op jit(solution)/shard_map/psum | solution.py:108
  (1138 shorter events, 1032.6 us)
Async XLA Ops:
  101.7 35.5 %all-gather.5.cloned.1.call-start = ((), (), s32[]{:S(2)}) async-start(), calls=%async_computation | async-start | bytes 2949120 | tf_op jit(solution)/shard_map/while/body/eval_jaxpr/all_gather | solution.py:53
  110.6 92.4 %all-gather.7.cloned.1.call-start = ((), (), s32[]{:S(2)}) async-start(), calls=%async_computation.1 | async-start | bytes 2949120 | tf_op jit(solution)/shard_map/while/body/eval_jaxpr/all_gather | solution.py:53
  233.6 10.0 collective-permute-start
  243.7 33.8 %all-gather.5.cloned.1.call-start = ((), (), s32[]{:S(2)}) async-start(), calls=%async_computation | async-start | bytes 2949120 | tf_op jit(solution)/shard_map/while/body/eval_jaxpr/all_gather | solution.py:53
  252.6 90.7 %all-gather.7.cloned.1.call-start = ((), (), s32[]{:S(2)}) async-start(), calls=%async_computation.1 | async-start | bytes 2949120 | tf_op jit(solution)/shard_map/while/body/eval_jaxpr/all_gather | solution.py:53
  384.0 33.8 %all-gather.5.cloned.1.call-start = ((), (), s32[]{:S(2)}) async-start(), calls=%async_computation | async-start | bytes 2949120 | tf_op jit(solution)/shard_map/while/body/eval_jaxpr/all_gather | solution.py:53
  392.9 90.7 %all-gather.7.cloned.1.call-start = ((), (), s32[]{:S(2)}) async-start(), calls=%async_computation.1 | async-start | bytes 2949120 | tf_op jit(solution)/shard_map/while/body/eval_jaxpr/all_gather | solution.py:53
  524.3 33.8 %all-gather.5.cloned.1.call-start = ((), (), s32[]{:S(2)}) async-start(), calls=%async_computation | async-start | bytes 2949120 | tf_op jit(solution)/shard_map/while/body/eval_jaxpr/all_gather | solution.py:53
  533.2 90.6 %all-gather.7.cloned.1.call-start = ((), (), s32[]{:S(2)}) async-start(), calls=%async_computation.1 | async-start | bytes 2949120 | tf_op jit(solution)/shard_map/while/body/eval_jaxpr/all_gather | solution.py:53
  654.5 10.0 collective-permute-start
  664.5 33.8 %all-gather.5.cloned.1.call-start = ((), (), s32[]{:S(2)}) async-start(), calls=%async_computation | async-start | bytes 2949120 | tf_op jit(solution)/shard_map/while/body/eval_jaxpr/all_gather | solution.py:53
  673.5 90.6 %all-gather.7.cloned.1.call-start = ((), (), s32[]{:S(2)}) async-start(), calls=%async_computation.1 | async-start | bytes 2949120 | tf_op jit(solution)/shard_map/while/body/eval_jaxpr/all_gather | solution.py:53
  794.8 10.0 collective-permute-start
  827.0 30.0 %all-gather.9.cloned.1.call-start = ((), (), s32[]{:S(2)}) async-start(), calls=%async_computation.2 | async-start | bytes 2949120 | tf_op jit(solution)/shard_map/while/body/eval_jaxpr/all_gather | solution.py:53
  836.0 86.8 %all-gather.11.cloned.1.call-start = ((), (), s32[]{:S(2)}) async-start(), calls=%async_computation.3 | async-start | bytes 2949120 | tf_op jit(solution)/shard_map/while/body/eval_jaxpr/all_gather | solution.py:53
  953.4 10.0 collective-permute-start.1
  963.5 33.8 %all-gather.9.cloned.1.call-start = ((), (), s32[]{:S(2)}) async-start(), calls=%async_computation.2 | async-start | bytes 2949120 | tf_op jit(solution)/shard_map/while/body/eval_jaxpr/all_gather | solution.py:53
  972.4 90.7 %all-gather.11.cloned.1.call-start = ((), (), s32[]{:S(2)}) async-start(), calls=%async_computation.3 | async-start | bytes 2949120 | tf_op jit(solution)/shard_map/while/body/eval_jaxpr/all_gather | solution.py:53
  1103.8 33.8 %all-gather.9.cloned.1.call-start = ((), (), s32[]{:S(2)}) async-start(), calls=%async_computation.2 | async-start | bytes 2949120 | tf_op jit(solution)/shard_map/while/body/eval_jaxpr/all_gather | solution.py:53
  1112.7 90.7 %all-gather.11.cloned.1.call-start = ((), (), s32[]{:S(2)}) async-start(), calls=%async_computation.3 | async-start | bytes 2949120 | tf_op jit(solution)/shard_map/while/body/eval_jaxpr/all_gather | solution.py:53
  1244.1 33.8 %all-gather.9.cloned.1.call-start = ((), (), s32[]{:S(2)}) async-start(), calls=%async_computation.2 | async-start | bytes 2949120 | tf_op jit(solution)/shard_map/while/body/eval_jaxpr/all_gather | solution.py:53
  1253.0 90.6 %all-gather.11.cloned.1.call-start = ((), (), s32[]{:S(2)}) async-start(), calls=%async_computation.3 | async-start | bytes 2949120 | tf_op jit(solution)/shard_map/while/body/eval_jaxpr/all_gather | solution.py:53
  1384.3 33.8 %all-gather.9.cloned.1.call-start = ((), (), s32[]{:S(2)}) async-start(), calls=%async_computation.2 | async-start | bytes 2949120 | tf_op jit(solution)/shard_map/while/body/eval_jaxpr/all_gather | solution.py:53
  1393.3 90.6 %all-gather.11.cloned.1.call-start = ((), (), s32[]{:S(2)}) async-start(), calls=%async_computation.3 | async-start | bytes 2949120 | tf_op jit(solution)/shard_map/while/body/eval_jaxpr/all_gather | solution.py:53
  (283 other events, 2959.6 us)
Sparse Core Ops, SparseCore 0:
  110.7 26.4 all-gather.4
  179.3 23.6 all-gather.6
  252.7 24.7 all-gather.4
  319.5 23.6 all-gather.6
  393.0 24.7 all-gather.4
  459.8 23.6 all-gather.6
  533.3 24.6 all-gather.4
  600.1 23.6 all-gather.6
  673.6 24.6 all-gather.4
  740.4 23.6 all-gather.6
  836.1 20.9 all-gather.8
  899.1 23.6 all-gather.10
  972.5 24.7 all-gather.8
  1039.3 23.6 all-gather.10
  1112.8 24.7 all-gather.8
  1179.6 23.6 all-gather.10
  1253.1 24.6 all-gather.8
  1319.9 23.6 all-gather.10
  1393.4 24.6 all-gather.8
  1460.2 23.6 all-gather.10
where the time goes:
time: 1560 us; the launch traced here: 1550 us
  matrix products  615 us (39%)
  waiting for transfers between devices  507 us (32%)
  local copies, waits for them, and re-layouts  231 us (15%)
  other arithmetic  109 us (7%)
  starting transfers between devices  36.1 us (2%)
  blocking collectives  20.4 us (1%)
  loops' own time  20.2 us (1%)
    all_gather x20, waiting for transfers between devices, run_layer(): lax.all_gather(qkv_rows[:, model_width:], 'sp', axis=0, tiled=True)  448 us
    dot_general x20, matrix products, run_layer(): jnp.dot(mlp_mid, down_stage[layer_j], preferred_element_type=jnp.float32)  185 us
    sub x20, matrix products, run_layer(): attn_prob = jax.nn.softmax(logits, axis=-1).astype(jnp.bfloat16)  159 us
    dot_general x20, matrix products, run_layer(): jnp.einsum('hrn,nhd->rhd', attn_prob, value_buf, preferred_element_type=j...  111 us
    dot_general x20, matrix products, run_layer(): jnp.dot(normed, qkv_stage[layer_j], preferred_element_type=jnp.float32)  94.2 us
    slice x40, local copies, waits for them, and re-layouts, run_layer(): key_new = kv_patch[:, :model_width].reshape(patch_rows, num_heads, head_dim)  80.6 us
    ppermute x10, waiting for transfers between devices, tick_body(): sent_rows = lax.ppermute(hidden, 'pp', forward_perm)  54.1 us
    dynamic_update_slice x20, other arithmetic, run_layer(): lax.dynamic_update_slice_in_dim(key_buf, jnp.where(is_valid, key_new, key...  43.9 us
  transfers between devices with their start and end apart: 31, of which 31 were waited for; matrix products, arithmetic and copies ran while one was open for 3% of the time, Pallas kernels for 0%

commit v1 on v0

v1 whole, which is shorter than its diff:
```python
import functools

import jax
import jax.numpy as jnp
from jax import lax
from jax.experimental import pallas as pl
from jax.experimental.pallas import tpu as pltpu
from jax.sharding import PartitionSpec as P

LN_EPS = 1e-6


def layer_norm(hidden):
    mean_val = jnp.mean(hidden, axis=-1, keepdims=True)
    centered = hidden - mean_val
    var_val = jnp.mean(centered * centered, axis=-1, keepdims=True)
    return centered * lax.rsqrt(var_val + LN_EPS)


def attend_kernel(head_dim, scale, q_ref, fresh_ref, kold_ref, vold_ref, out_ref):
    half = fresh_ref.shape[0] // 2
    first = pl.program_id(0) < pl.num_programs(0) // 2
    query = q_ref[:, :head_dim]
    key0 = fresh_ref[:half, head_dim:2 * head_dim]
    val0 = fresh_ref[:half, 2 * head_dim:]
    key1 = jnp.where(first, kold_ref[...], fresh_ref[half:, head_dim:2 * head_dim])
    val1 = jnp.where(first, vold_ref[...], fresh_ref[half:, 2 * head_dim:])
    dims = (((1,), (1,)), ((), ()))
    logit0 = lax.dot_general(query, key0, dims, preferred_element_type=jnp.float32) * scale
    logit1 = lax.dot_general(query, key1, dims, preferred_element_type=jnp.float32) * scale
    peak = jnp.maximum(jnp.max(logit0, axis=-1, keepdims=True), jnp.max(logit1, axis=-1, keepdims=True))
    exp0 = jnp.exp(logit0 - peak)
    exp1 = jnp.exp(logit1 - peak)
    total = jnp.sum(exp0, axis=-1, keepdims=True) + jnp.sum(exp1, axis=-1, keepdims=True)
    inv = 1.0 / total
    prob0 = (exp0 * inv).astype(jnp.bfloat16)
    prob1 = (exp1 * inv).astype(jnp.bfloat16)
    out = jnp.dot(prob0, val0, preferred_element_type=jnp.float32) + jnp.dot(prob1, val1, preferred_element_type=jnp.float32)
    out_ref[...] = out.astype(jnp.bfloat16)


def solution(mesh):
    stage_count = mesh.shape["pp"]
    split_count = mesh.shape["sp"]
    group = stage_count * split_count
    axes = ("pp", "sp")
    row_spec = P("dp", "sp", None)
    full_spec = P()
    buf_spec = P("dp", None, None, None)
    in_specs = (row_spec, P(None, "sp", None), P("dp", None), P("dp"), full_spec, full_spec, full_spec, full_spec, full_spec, full_spec, full_spec, full_spec, full_spec, full_spec, buf_spec, buf_spec)

    def device_fn(latent_in, pos_embed, condition, step_size, w_in, w_ada, w_qkv, w_o, w_up, w_down, b_layer, w_fa, b_fa, w_out, k_old, v_old):
        num_patches, sub_rows, _ = latent_in.shape
        width = w_in.shape[1]
        layers = w_qkv.shape[0]
        heads, head_dim = k_old.shape[2], k_old.shape[3]
        tokens = k_old.shape[1]
        patch_rows = tokens // num_patches
        per_patch = stage_count // num_patches
        rows = sub_rows // per_patch
        stage_idx = lax.axis_index("pp")
        me = stage_idx * split_count + lax.axis_index("sp")
        patch = stage_idx // per_patch
        start = (stage_idx % per_patch) * rows
        latent = lax.dynamic_slice(latent_in, (patch, start, 0), (1, rows, latent_in.shape[2]))[0]
        pos = lax.dynamic_slice(pos_embed, (patch, start, 0), (1, rows, width))[0].astype(jnp.float32)
        keys1 = lax.dynamic_slice(k_old, (0, patch_rows, me, 0), (layers, patch_rows, 1, head_dim))[:, :, 0]
        vals1 = lax.dynamic_slice(v_old, (0, patch_rows, me, 0), (layers, patch_rows, 1, head_dim))[:, :, 0]
        bias = b_layer.astype(jnp.float32)

        cond = jax.nn.silu(condition.astype(jnp.float32)).astype(jnp.bfloat16)
        pieces = group // layers
        piece = 6 * width // pieces
        w_mine = lax.dynamic_slice(w_ada, (me // pieces, 0, (me % pieces) * piece), (1, width, piece))[0]
        mod_mine = jnp.dot(cond, w_mine, preferred_element_type=jnp.float32)
        mod_all = lax.all_gather(mod_mine, axes, axis=0, tiled=False)
        mod_all = mod_all.reshape(layers, pieces, 2, piece).transpose(2, 0, 1, 3).reshape(2, layers, 6 * width) + bias[None, :, :6 * width]
        final_mod = jnp.dot(cond, w_fa, preferred_element_type=jnp.float32) + b_fa.astype(jnp.float32)

        blocks = 4
        attend = pl.pallas_call(
            functools.partial(attend_kernel, head_dim, head_dim ** -0.5),
            grid=(blocks,),
            out_shape=jax.ShapeDtypeStruct((tokens, head_dim), jnp.bfloat16),
            in_specs=[
                pl.BlockSpec((tokens // blocks, 3 * head_dim), lambda i: (i, 0)),
                pl.BlockSpec((tokens, 3 * head_dim), lambda i: (0, 0)),
                pl.BlockSpec((patch_rows, head_dim), lambda i: (0, 0)),
                pl.BlockSpec((patch_rows, head_dim), lambda i: (0, 0)),
            ],
            out_specs=pl.BlockSpec((tokens // blocks, head_dim), lambda i: (i, 0)),
            cost_estimate=pl.CostEstimate(flops=4 * tokens * tokens * head_dim, bytes_accessed=2 * tokens * 4 * head_dim, transcendentals=tokens * tokens),
        )

        keys1 = [keys1[layer] for layer in range(layers)]
        vals1 = [vals1[layer] for layer in range(layers)]
        for step in range(2):
            hidden = (jnp.dot(latent.astype(jnp.bfloat16), w_in, preferred_element_type=jnp.float32) + pos).astype(jnp.bfloat16)
            for layer in range(layers):
                row = bias[layer]
                s1, b1, g1, s2, b2, g2 = jnp.split(mod_all[step, layer], 6)
                normed = (layer_norm(hidden.astype(jnp.float32)) * (1.0 + s1) + b1).astype(jnp.bfloat16)
                qkv = (jnp.dot(normed, w_qkv[layer], preferred_element_type=jnp.float32) + row[6 * width:9 * width]).astype(jnp.bfloat16)
                send = qkv.reshape(rows, 3, heads, head_dim).transpose(2, 0, 1, 3).reshape(heads, rows, 3 * head_dim)
                fresh = lax.all_to_all(send, axes, split_axis=0, concat_axis=0, tiled=True).reshape(tokens, 3 * head_dim)
                out = attend(fresh, fresh, keys1[layer], vals1[layer])
                keys1[layer] = fresh[patch_rows:, head_dim:2 * head_dim]
                vals1[layer] = fresh[patch_rows:, 2 * head_dim:]
                back = lax.all_to_all(out.reshape(group, rows, head_dim), axes, split_axis=0, concat_axis=0, tiled=True)
                attn = back.transpose(1, 0, 2).reshape(rows, width)
                resid = hidden.astype(jnp.float32) + g1 * (jnp.dot(attn, w_o[layer], preferred_element_type=jnp.float32) + row[9 * width:10 * width])
                mlp_in = (layer_norm(resid) * (1.0 + s2) + b2).astype(jnp.bfloat16)
                mid = jax.nn.gelu(jnp.dot(mlp_in, w_up[layer], preferred_element_type=jnp.float32) + row[10 * width:14 * width], approximate=True).astype(jnp.bfloat16)
                hidden = (resid + g2 * (jnp.dot(mid, w_down[layer], preferred_element_type=jnp.float32) + row[14 * width:])).astype(jnp.bfloat16)
            s_out, b_out = jnp.split(final_mod[step], 2)
            normed = (layer_norm(hidden.astype(jnp.float32)) * (1.0 + s_out) + b_out).astype(jnp.bfloat16)
            latent = latent + step_size[step] * jnp.dot(normed, w_out, preferred_element_type=jnp.float32)
        return lax.all_gather(latent, "pp", axis=0, tiled=False).reshape(num_patches, sub_rows, latent.shape[-1])

    return jax.shard_map(device_fn, mesh=mesh, in_specs=in_specs, out_specs=row_spec, check_vma=False)
```

time: 1560 us -> 1010 us (0.65)
  matrix products: 615 us -> 274 us
  waiting for transfers between devices: 507 us -> 254 us
  blocking collectives: 20.4 us -> 179 us
  local copies, waits for them, and re-layouts: 231 us -> 96.9 us
  Pallas kernels: 0 us -> 99.3 us
  other arithmetic: 109 us -> 10.7 us
  starting transfers between devices: 36.1 us -> 85.1 us
  loops' own time: 20.2 us -> 0 us
    all_gather x20 -> x0, waiting for transfers between devices: 448 us -> none  [run_layer(): lax.all_gather(qkv_rows[:, model_width:], 'sp', axis=0, tiled=True)]
    all_to_all x0 -> x22, waiting for transfers between devices: none -> 254 us  [the longest x16 202 us: device_fn(): lax.all_to_all(send, axes, split_axis=0, concat_axis=0, tiled=True)]
    dot_general x104 -> x54, matrix products: 455 us -> 274 us  [the longest x16 148 us: device_fn(): jnp.dot(mid, w_down[layer], preferred_element_type=jnp.float32)]
    sub x20 -> x0, matrix products: 159 us -> none  [run_layer(): attn_prob = jax.nn.softmax(logits, axis=-1).astype(jnp.bfloat16)]
    all_to_all x0 -> x10, blocking collectives: none -> 142 us  [device_fn(): lax.all_to_all(out.reshape(group, rows, head_dim), axes, split_axis=0, co...]
    slice x151 -> x14, local copies, waits for them, and re-layouts: 145 us -> 13 us  [the longest x8 6.73 us: device_fn(): vals1[layer] = fresh[patch_rows:, 2 * head_dim:]]
    pallas_call x0 -> x16, Pallas kernels: none -> 99.3 us  [device_fn(): out = attend(fresh, fresh, keys1[layer], vals1[layer])]
    all_to_all x0 -> x22, starting transfers between devices: none -> 85.1 us  [the longest x16 58.8 us: device_fn(): lax.all_to_all(send, axes, split_axis=0, concat_axis=0, tiled=True)]
  transfers between devices with their start and end apart: 31 -> 22, of which waited for: 31 -> 22; matrix products, arithmetic and copies ran while one was open for 3% -> 3% of each run, Pallas kernels for 0% -> 0%
where the time goes in v1:
time: 1010 us; the launch traced here: 1000 us
  matrix products  274 us (27%)
  waiting for transfers between devices  254 us (25%)
  blocking collectives  179 us (18%)
  Pallas kernels  99.3 us (10%)
  local copies, waits for them, and re-layouts  96.9 us (10%)
  starting transfers between devices  85.1 us (8%)
  other arithmetic  10.7 us (1%)
    all_to_all x16, waiting for transfers between devices, device_fn(): lax.all_to_all(send, axes, split_axis=0, concat_axis=0, tiled=True)  202 us
    dot_general x16, matrix products, device_fn(): jnp.dot(mid, w_down[layer], preferred_element_type=jnp.float32)  148 us
    all_to_all x10, blocking collectives, device_fn(): lax.all_to_all(out.reshape(group, rows, head_dim), axes, split_axis=0, co...  142 us
    pallas_call x16, Pallas kernels, device_fn(): out = attend(fresh, fresh, keys1[layer], vals1[layer])  99.3 us
    dot_general x16, matrix products, device_fn(): jnp.dot(normed, w_qkv[layer], preferred_element_type=jnp.float32)  74.8 us
    all_to_all x16, starting transfers between devices, device_fn(): lax.all_to_all(send, axes, split_axis=0, concat_axis=0, tiled=True)  58.8 us
    all_to_all x6, waiting for transfers between devices, device_fn(): lax.all_to_all(out.reshape(group, rows, head_dim), axes, split_axis=0, co...  51.3 us
    reshape x48, local copies, waits for them, and re-layouts, device_fn(): qkv.reshape(rows, 3, heads, head_dim).transpose(2, 0, 1, 3)  49.8 us
  transfers between devices with their start and end apart: 22, of which 22 were waited for; matrix products, arithmetic and copies ran while one was open for 3% of the time, Pallas kernels for 0%

profile of v1, /device:TPU:0, one launch (start us, length us, event | category | flops | bytes accessed | tf_op | source)
XLA Modules:
  0.0 1001.8 jit_solution(7506337687446291557)
XLA Ops:
  8.0 24.3 %all-gather.2 = f32[16,2,3456]{2,1,0:T(2,128)S(1)} all-gather(f32[1,2,3456]{2,1,0:T(2,128)S(1)} %fusion.291), channel_id=2, replica_groups=mesh['dp'=2,'pp'=4,'sp'=4] {'pp','sp'}, dimensions={0}, use_global_device_ids=true | all-gather | bytes 470016 | tf_op jit(solution)/shard_map/all_gather | solution.py:76
  106.9 12.5 %all-to-all-done.2 = bf16[16,64,216]{2,1,0:T(8,128)(2,1)S(1)} async-done(((bf16[16,64,216]{2,1,0:T(8,128)(2,1)}), bf16[16,64,216]{2,1,0:T(8,128)(2,1)S(1)}, u32[]{:S(2)}, u32[]{:S(2)}) %all-to-all-start.2) | async-done | bytes 442400 | tf_op jit(solution)/shard_map/all_to_all | solution.py:105
  126.4 14.5 %all_to_all.160 = bf16[16,64,72]{2,1,0:T(8,128)(2,1)S(1)} all-to-all(bf16[16,64,72]{2,1,0:T(8,128)(2,1)} %bitcast.950), channel_id=1, replica_groups=mesh['dp'=2,'pp'=4,'sp'=4] {'pp','sp'}, dimensions={0} | all-to-all | bytes 294912 | tf_op jit(solution)/shard_map/all_to_all | solution.py:109
  166.7 12.5 %all-to-all-done.4 = bf16[16,64,216]{2,1,0:T(8,128)(2,1)S(1)} async-done(((bf16[16,64,216]{2,1,0:T(8,128)(2,1)}), bf16[16,64,216]{2,1,0:T(8,128)(2,1)S(1)}, u32[]{:S(2)}, u32[]{:S(2)}) %all-to-all-start.4) | async-done | bytes 442400 | tf_op jit(solution)/shard_map/all_to_all | solution.py:105
  226.1 12.5 %all-to-all-done.6 = bf16[16,64,216]{2,1,0:T(8,128)(2,1)S(1)} async-done(((bf16[16,64,216]{2,1,0:T(8,128)(2,1)}), bf16[16,64,216]{2,1,0:T(8,128)(2,1)S(1)}, u32[]{:S(2)}, u32[]{:S(2)}) %all-to-all-start.6) | async-done | bytes 442400 | tf_op jit(solution)/shard_map/all_to_all | solution.py:105
  245.6 14.2 %all_to_all.161 = bf16[16,64,72]{2,1,0:T(8,128)(2,1)S(1)} all-to-all(bf16[16,64,72]{2,1,0:T(8,128)(2,1)} %bitcast.951), channel_id=1, replica_groups=mesh['dp'=2,'pp'=4,'sp'=4] {'pp','sp'}, dimensions={0} | all-to-all | bytes 294912 | tf_op jit(solution)/shard_map/all_to_all | solution.py:109
  305.1 14.2 %all_to_all.162 = bf16[16,64,72]{2,1,0:T(8,128)(2,1)S(1)} all-to-all(bf16[16,64,72]{2,1,0:T(8,128)(2,1)} %bitcast.952), channel_id=1, replica_groups=mesh['dp'=2,'pp'=4,'sp'=4] {'pp','sp'}, dimensions={0} | all-to-all | bytes 294912 | tf_op jit(solution)/shard_map/all_to_all | solution.py:109
  364.5 14.3 %all_to_all.163 = bf16[16,64,72]{2,1,0:T(8,128)(2,1)S(1)} all-to-all(bf16[16,64,72]{2,1,0:T(8,128)(2,1)} %bitcast.953), channel_id=1, replica_groups=mesh['dp'=2,'pp'=4,'sp'=4] {'pp','sp'}, dimensions={0} | all-to-all | bytes 294912 | tf_op jit(solution)/shard_map/all_to_all | solution.py:109
  404.5 12.5 %all-to-all-done.12 = bf16[16,64,216]{2,1,0:T(8,128)(2,1)S(1)} async-done(((bf16[16,64,216]{2,1,0:T(8,128)(2,1)}), bf16[16,64,216]{2,1,0:T(8,128)(2,1)S(1)}, u32[]{:S(2)}, u32[]{:S(2)}) %all-to-all-start.12) | async-done | bytes 442400 | tf_op jit(solution)/shard_map/all_to_all | solution.py:105
  524.9 13.1 %all-to-all-done.16 = bf16[16,64,216]{2,1,0:T(8,128)(2,1)S(1)} async-done(((bf16[16,64,216]{2,1,0:T(8,128)(2,1)}), bf16[16,64,216]{2,1,0:T(8,128)(2,1)S(1)}, u32[]{:S(2)}, u32[]{:S(2)}) %all-to-all-start.16) | async-done | bytes 442400 | tf_op jit(solution)/shard_map/all_to_all | solution.py:105
  545.0 14.2 %all_to_all.164 = bf16[16,64,72]{2,1,0:T(8,128)(2,1)S(1)} all-to-all(bf16[16,64,72]{2,1,0:T(8,128)(2,1)} %bitcast.944), channel_id=1, replica_groups=mesh['dp'=2,'pp'=4,'sp'=4] {'pp','sp'}, dimensions={0} | all-to-all | bytes 294912 | tf_op jit(solution)/shard_map/all_to_all | solution.py:109
  584.2 13.1 %all-to-all-done.18 = bf16[16,64,216]{2,1,0:T(8,128)(2,1)S(1)} async-done(((bf16[16,64,216]{2,1,0:T(8,128)(2,1)}), bf16[16,64,216]{2,1,0:T(8,128)(2,1)S(1)}, u32[]{:S(2)}, u32[]{:S(2)}) %all-to-all-start.18) | async-done | bytes 442400 | tf_op jit(solution)/shard_map/all_to_all | solution.py:105
  643.6 13.1 %all-to-all-done.20 = bf16[16,64,216]{2,1,0:T(8,128)(2,1)S(1)} async-done(((bf16[16,64,216]{2,1,0:T(8,128)(2,1)}), bf16[16,64,216]{2,1,0:T(8,128)(2,1)S(1)}, u32[]{:S(2)}, u32[]{:S(2)}) %all-to-all-start.20) | async-done | bytes 442400 | tf_op jit(solution)/shard_map/all_to_all | solution.py:105
  663.7 14.2 %all_to_all.165 = bf16[16,64,72]{2,1,0:T(8,128)(2,1)S(1)} all-to-all(bf16[16,64,72]{2,1,0:T(8,128)(2,1)} %bitcast.945), channel_id=1, replica_groups=mesh['dp'=2,'pp'=4,'sp'=4] {'pp','sp'}, dimensions={0} | all-to-all | bytes 294912 | tf_op jit(solution)/shard_map/all_to_all | solution.py:109
  703.0 13.1 %all-to-all-done.22 = bf16[16,64,216]{2,1,0:T(8,128)(2,1)S(1)} async-done(((bf16[16,64,216]{2,1,0:T(8,128)(2,1)}), bf16[16,64,216]{2,1,0:T(8,128)(2,1)S(1)}, u32[]{:S(2)}, u32[]{:S(2)}) %all-to-all-start.22) | async-done | bytes 442400 | tf_op jit(solution)/shard_map/all_to_all | solution.py:105
  723.2 14.5 %all_to_all.166 = bf16[16,64,72]{2,1,0:T(8,128)(2,1)S(1)} all-to-all(bf16[16,64,72]{2,1,0:T(8,128)(2,1)} %bitcast.946), channel_id=1, replica_groups=mesh['dp'=2,'pp'=4,'sp'=4] {'pp','sp'}, dimensions={0} | all-to-all | bytes 294912 | tf_op jit(solution)/shard_map/all_to_all | solution.py:109
  762.7 13.1 %all-to-all-done.24 = bf16[16,64,216]{2,1,0:T(8,128)(2,1)S(1)} async-done(((bf16[16,64,216]{2,1,0:T(8,128)(2,1)}), bf16[16,64,216]{2,1,0:T(8,128)(2,1)S(1)}, u32[]{:S(2)}, u32[]{:S(2)}) %all-to-all-start.24) | async-done | bytes 442400 | tf_op jit(solution)/shard_map/all_to_all | solution.py:105
  822.0 13.1 %all-to-all-done.26 = bf16[16,64,216]{2,1,0:T(8,128)(2,1)S(1)} async-done(((bf16[16,64,216]{2,1,0:T(8,128)(2,1)}), bf16[16,64,216]{2,1,0:T(8,128)(2,1)S(1)}, u32[]{:S(2)}, u32[]{:S(2)}) %all-to-all-start.26) | async-done | bytes 442400 | tf_op jit(solution)/shard_map/all_to_all | solution.py:105
  842.2 14.1 %all_to_all.167 = bf16[16,64,72]{2,1,0:T(8,128)(2,1)S(1)} all-to-all(bf16[16,64,72]{2,1,0:T(8,128)(2,1)} %bitcast.947), channel_id=1, replica_groups=mesh['dp'=2,'pp'=4,'sp'=4] {'pp','sp'}, dimensions={0} | all-to-all | bytes 294912 | tf_op jit(solution)/shard_map/all_to_all | solution.py:109
  881.3 13.1 %all-to-all-done.28 = bf16[16,64,216]{2,1,0:T(8,128)(2,1)S(1)} async-done(((bf16[16,64,216]{2,1,0:T(8,128)(2,1)}), bf16[16,64,216]{2,1,0:T(8,128)(2,1)S(1)}, u32[]{:S(2)}, u32[]{:S(2)}) %all-to-all-start.28) | async-done | bytes 442400 | tf_op jit(solution)/shard_map/all_to_all | solution.py:105
  901.4 14.0 %all_to_all.168 = bf16[16,64,72]{2,1,0:T(8,128)(2,1)S(1)} all-to-all(bf16[16,64,72]{2,1,0:T(8,128)(2,1)} %bitcast.948), channel_id=1, replica_groups=mesh['dp'=2,'pp'=4,'sp'=4] {'pp','sp'}, dimensions={0} | all-to-all | bytes 294912 | tf_op jit(solution)/shard_map/all_to_all | solution.py:109
  940.3 13.1 %all-to-all-done.30 = bf16[16,64,216]{2,1,0:T(8,128)(2,1)S(1)} async-done(((bf16[16,64,216]{2,1,0:T(8,128)(2,1)}), bf16[16,64,216]{2,1,0:T(8,128)(2,1)S(1)}, u32[]{:S(2)}, u32[]{:S(2)}) %all-to-all-start.30) | async-done | bytes 442400 | tf_op jit(solution)/shard_map/all_to_all | solution.py:105
  960.5 13.8 %all_to_all.169 = bf16[16,64,72]{2,1,0:T(8,128)(2,1)S(1)} all-to-all(bf16[16,64,72]{2,1,0:T(8,128)(2,1)} %bitcast.949), channel_id=1, replica_groups=mesh['dp'=2,'pp'=4,'sp'=4] {'pp','sp'}, dimensions={0} | all-to-all | bytes 294912 | tf_op jit(solution)/shard_map/all_to_all | solution.py:109
  987.8 13.1 %all-gather.3 = f32[4,64,16]{1,2,0:T(8,128)S(1)} all-gather(f32[1,64,16]{1,2,0:T(8,128)S(1)} %fusion.923), channel_id=3, replica_groups=mesh['dp'=2,'pp'=4,'sp'=4] {'pp'}, dimensions={0}, use_global_device_ids=true | all-gather | bytes 20480 | tf_op jit(solution)/shard_map/all_gather | solution.py:118
  (585 shorter events, 664.7 us)
Async XLA Ops:
  42.4 17.6 %all-to-all-start = ((bf16[16,64,216]{2,1,0:T(8,128)(2,1)}), bf16[16,64,216]{2,1,0:T(8,128)(2,1)S(1)}, u32[]{:S(2)}, u32[]{:S(2)}) async-start(bf16[16,64,216]{2,1,0:T(8,128)(2,1)} %reshape.1214), calls=%async_computation | async-start | bytes 1048576 | tf_op jit(solution)/shard_map/all_to_all | solution.py:105
  67.0 14.1 %all-to-all-start.1 = ((bf16[16,64,72]{2,1,0:T(8,128)(2,1)}), bf16[16,64,72]{2,1,0:T(8,128)(2,1)S(1)}, u32[]{:S(2)}, u32[]{:S(2)}) async-start(bf16[16,64,72]{2,1,0:T(8,128)(2,1)} %bitcast.938), calls=%async_computation.1 | async-start | bytes 524288 | tf_op jit(solution)/shard_map/all_to_all | solution.py:109
  101.7 39.7 %copy-start.85 = (f32[1152]{0:T(1024)S(1)}, f32[1152]{0:T(1024)}, u32[]{:S(2)}) copy-start(f32[1152]{0:T(1024)} %get-tuple-element.18) | copy-start | bytes 13828
  101.7 39.7 %copy-start.106 = (f32[1152]{0:T(1024)S(1)}, f32[1152]{0:T(1024)}, u32[]{:S(2)}) copy-start(f32[1152]{0:T(1024)} %get-tuple-element.126) | copy-start | bytes 13828
  101.7 17.7 %all-to-all-start.2 = ((bf16[16,64,216]{2,1,0:T(8,128)(2,1)}), bf16[16,64,216]{2,1,0:T(8,128)(2,1)S(1)}, u32[]{:S(2)}, u32[]{:S(2)}) async-start(bf16[16,64,216]{2,1,0:T(8,128)(2,1)} %reshape.1219), calls=%async_computation.2 | async-start | bytes 1048576 | tf_op jit(solution)/shard_map/all_to_all | solution.py:105
  161.5 17.7 %all-to-all-start.4 = ((bf16[16,64,216]{2,1,0:T(8,128)(2,1)}), bf16[16,64,216]{2,1,0:T(8,128)(2,1)S(1)}, u32[]{:S(2)}, u32[]{:S(2)}) async-start(bf16[16,64,216]{2,1,0:T(8,128)(2,1)} %reshape.1224), calls=%async_computation.4 | async-start | bytes 1048576 | tf_op jit(solution)/shard_map/all_to_all | solution.py:105
  186.2 14.1 %all-to-all-start.5 = ((bf16[16,64,72]{2,1,0:T(8,128)(2,1)}), bf16[16,64,72]{2,1,0:T(8,128)(2,1)S(1)}, u32[]{:S(2)}, u32[]{:S(2)}) async-start(bf16[16,64,72]{2,1,0:T(8,128)(2,1)} %bitcast.941), calls=%async_computation.5 | async-start | bytes 524288 | tf_op jit(solution)/shard_map/all_to_all | solution.py:109
  220.8 17.7 %all-to-all-start.6 = ((bf16[16,64,216]{2,1,0:T(8,128)(2,1)}), bf16[16,64,216]{2,1,0:T(8,128)(2,1)S(1)}, u32[]{:S(2)}, u32[]{:S(2)}) async-start(bf16[16,64,216]{2,1,0:T(8,128)(2,1)} %reshape.1229), calls=%async_computation.6 | async-start | bytes 1048576 | tf_op jit(solution)/shard_map/all_to_all | solution.py:105
  280.4 17.7 %all-to-all-start.8 = ((bf16[16,64,216]{2,1,0:T(8,128)(2,1)}), bf16[16,64,216]{2,1,0:T(8,128)(2,1)S(1)}, u32[]{:S(2)}, u32[]{:S(2)}) async-start(bf16[16,64,216]{2,1,0:T(8,128)(2,1)} %reshape.1234), calls=%async_computation.8 | async-start | bytes 1048576 | tf_op jit(solution)/shard_map/all_to_all | solution.py:105
  339.8 17.7 %all-to-all-start.10 = ((bf16[16,64,216]{2,1,0:T(8,128)(2,1)}), bf16[16,64,216]{2,1,0:T(8,128)(2,1)S(1)}, u32[]{:S(2)}, u32[]{:S(2)}) async-start(bf16[16,64,216]{2,1,0:T(8,128)(2,1)} %reshape.1239), calls=%async_computation.10 | async-start | bytes 1048576 | tf_op jit(solution)/shard_map/all_to_all | solution.py:105
  399.3 17.7 %all-to-all-start.12 = ((bf16[16,64,216]{2,1,0:T(8,128)(2,1)}), bf16[16,64,216]{2,1,0:T(8,128)(2,1)S(1)}, u32[]{:S(2)}, u32[]{:S(2)}) async-start(bf16[16,64,216]{2,1,0:T(8,128)(2,1)} %reshape.1244), calls=%async_computation.12 | async-start | bytes 1048576 | tf_op jit(solution)/shard_map/all_to_all | solution.py:105
  424.0 14.5 %all-to-all-start.13 = ((bf16[16,64,72]{2,1,0:T(8,128)(2,1)}), bf16[16,64,72]{2,1,0:T(8,128)(2,1)S(1)}, u32[]{:S(2)}, u32[]{:S(2)}) async-start(bf16[16,64,72]{2,1,0:T(8,128)(2,1)} %bitcast.942), calls=%async_computation.13 | async-start | bytes 524288 | tf_op jit(solution)/shard_map/all_to_all | solution.py:109
  458.9 17.6 %all-to-all-start.14 = ((bf16[16,64,216]{2,1,0:T(8,128)(2,1)}), bf16[16,64,216]{2,1,0:T(8,128)(2,1)S(1)}, u32[]{:S(2)}, u32[]{:S(2)}) async-start(bf16[16,64,216]{2,1,0:T(8,128)(2,1)} %reshape.1249), calls=%async_computation.14 | async-start | bytes 1048576 | tf_op jit(solution)/shard_map/all_to_all | solution.py:105
  483.5 14.0 %all-to-all-start.15 = ((bf16[16,64,72]{2,1,0:T(8,128)(2,1)}), bf16[16,64,72]{2,1,0:T(8,128)(2,1)S(1)}, u32[]{:S(2)}, u32[]{:S(2)}) async-start(bf16[16,64,72]{2,1,0:T(8,128)(2,1)} %bitcast.943), calls=%async_computation.15 | async-start | bytes 524288 | tf_op jit(solution)/shard_map/all_to_all | solution.py:109
  520.3 17.7 %all-to-all-start.16 = ((bf16[16,64,216]{2,1,0:T(8,128)(2,1)}), bf16[16,64,216]{2,1,0:T(8,128)(2,1)S(1)}, u32[]{:S(2)}, u32[]{:S(2)}) async-start(bf16[16,64,216]{2,1,0:T(8,128)(2,1)} %reshape.1254), calls=%async_computation.16 | async-start | bytes 1048576 | tf_op jit(solution)/shard_map/all_to_all | solution.py:105
  579.6 17.7 %all-to-all-start.18 = ((bf16[16,64,216]{2,1,0:T(8,128)(2,1)}), bf16[16,64,216]{2,1,0:T(8,128)(2,1)S(1)}, u32[]{:S(2)}, u32[]{:S(2)}) async-start(bf16[16,64,216]{2,1,0:T(8,128)(2,1)} %reshape.1259), calls=%async_computation.18 | async-start | bytes 1048576 | tf_op jit(solution)/shard_map/all_to_all | solution.py:105
  604.3 14.2 %all-to-all-start.19 = ((bf16[16,64,72]{2,1,0:T(8,128)(2,1)}), bf16[16,64,72]{2,1,0:T(8,128)(2,1)S(1)}, u32[]{:S(2)}, u32[]{:S(2)}) async-start(bf16[16,64,72]{2,1,0:T(8,128)(2,1)} %bitcast.940), calls=%async_computation.19 | async-start | bytes 524288 | tf_op jit(solution)/shard_map/all_to_all | solution.py:109
  639.0 17.7 %all-to-all-start.20 = ((bf16[16,64,216]{2,1,0:T(8,128)(2,1)}), bf16[16,64,216]{2,1,0:T(8,128)(2,1)S(1)}, u32[]{:S(2)}, u32[]{:S(2)}) async-start(bf16[16,64,216]{2,1,0:T(8,128)(2,1)} %reshape.1264), calls=%async_computation.20 | async-start | bytes 1048576 | tf_op jit(solution)/shard_map/all_to_all | solution.py:105
  698.4 17.7 %all-to-all-start.22 = ((bf16[16,64,216]{2,1,0:T(8,128)(2,1)}), bf16[16,64,216]{2,1,0:T(8,128)(2,1)S(1)}, u32[]{:S(2)}, u32[]{:S(2)}) async-start(bf16[16,64,216]{2,1,0:T(8,128)(2,1)} %reshape.1269), calls=%async_computation.22 | async-start | bytes 1048576 | tf_op jit(solution)/shard_map/all_to_all | solution.py:105
  758.2 17.7 %all-to-all-start.24 = ((bf16[16,64,216]{2,1,0:T(8,128)(2,1)}), bf16[16,64,216]{2,1,0:T(8,128)(2,1)S(1)}, u32[]{:S(2)}, u32[]{:S(2)}) async-start(bf16[16,64,216]{2,1,0:T(8,128)(2,1)} %reshape.1274), calls=%async_computation.24 | async-start | bytes 1048576 | tf_op jit(solution)/shard_map/all_to_all | solution.py:105
  782.9 14.1 %all-to-all-start.25 = ((bf16[16,64,72]{2,1,0:T(8,128)(2,1)}), bf16[16,64,72]{2,1,0:T(8,128)(2,1)S(1)}, u32[]{:S(2)}, u32[]{:S(2)}) async-start(bf16[16,64,72]{2,1,0:T(8,128)(2,1)} %bitcast.939), calls=%async_computation.25 | async-start | bytes 524288 | tf_op jit(solution)/shard_map/all_to_all | solution.py:109
  817.4 17.7 %all-to-all-start.26 = ((bf16[16,64,216]{2,1,0:T(8,128)(2,1)}), bf16[16,64,216]{2,1,0:T(8,128)(2,1)S(1)}, u32[]{:S(2)}, u32[]{:S(2)}) async-start(bf16[16,64,216]{2,1,0:T(8,128)(2,1)} %reshape.1279), calls=%async_computation.26 | async-start | bytes 1048576 | tf_op jit(solution)/shard_map/all_to_all | solution.py:105
  876.7 17.7 %all-to-all-start.28 = ((bf16[16,64,216]{2,1,0:T(8,128)(2,1)}), bf16[16,64,216]{2,1,0:T(8,128)(2,1)S(1)}, u32[]{:S(2)}, u32[]{:S(2)}) async-start(bf16[16,64,216]{2,1,0:T(8,128)(2,1)} %reshape.1284), calls=%async_computation.28 | async-start | bytes 1048576 | tf_op jit(solution)/shard_map/all_to_all | solution.py:105
  935.9 17.6 %all-to-all-start.30 = ((bf16[16,64,216]{2,1,0:T(8,128)(2,1)}), bf16[16,64,216]{2,1,0:T(8,128)(2,1)S(1)}, u32[]{:S(2)}, u32[]{:S(2)}) async-start(bf16[16,64,216]{2,1,0:T(8,128)(2,1)} %reshape.1289), calls=%async_computation.30 | async-start | bytes 1048576 | tf_op jit(solution)/shard_map/all_to_all | solution.py:105
  (126 other events, 1880.1 us)

commit v2 on v1

v2 whole, which is shorter than its diff:
```python
import functools
import math

import jax
import jax.numpy as jnp
from jax import lax
from jax.experimental import pallas as pl
from jax.experimental.pallas import tpu as pltpu
from jax.sharding import PartitionSpec as P

LN_EPS = 1e-6
GROUP = 16
MESH = pl.DeviceIdType.MESH
ORDER = (15, 7, 14, 6, 13, 5, 12, 4, 11, 3, 10, 2, 9, 8, 1)


def layer_norm(hidden):
    mean_val = jnp.mean(hidden, axis=-1, keepdims=True)
    centered = hidden - mean_val
    var_val = jnp.mean(centered * centered, axis=-1, keepdims=True)
    return centered * lax.rsqrt(var_val + LN_EPS)


def step_kernel(dims, latent_ref, pos_ref, step_ref, w_in_ref, w_out_ref, mod_ref, fin_ref, bias_ref, kv_ref, w_qkv, w_o, w_up, w_down, out_ref,
                wq_v, wo_v, wu_v, wd_v, mods, cache, send, recv, obuf, back, qkv, attn, mid, hid, resid, xbuf, xall,
                w_sem, kv_sem, m_send, m_recv, q_send, q_recv, o_send, o_recv, x_send, x_recv):
    rows, width, layers, head_dim = dims
    bf16, f32 = jnp.bfloat16, jnp.float32
    dp, pp, sp = lax.axis_index("dp"), lax.axis_index("pp"), lax.axis_index("sp")
    zc, yc, cc = pp % 2, sp // 2, sp % 2
    image = pp // 2
    me = dp * 8 + zc * 4 + sp

    def peer_of(d):
        x, z, y, c = (dp + d // 8) % 2, (zc + (d // 4) % 2) % 2, (yc + (d // 2) % 2) % 2, (cc + d % 2) % 2
        s = y * 2 + c
        return x * 8 + z * 4 + s, (x, image * 2 + z, s)

    def place_of(g):
        return (g // 8, image * 2 + (g // 4) % 2, g % 4)

    barrier = pltpu.get_barrier_semaphore()
    for d in ORDER:
        pl.semaphore_signal(barrier, inc=1, device_id=peer_of(d)[1], device_id_type=MESH)
    for k in range(4):
        pl.semaphore_signal(barrier, inc=1, device_id=(k // 2, (1 - image) * 2 + k % 2, sp), device_id_type=MESH)

    def load(k, src, dst):
        return pltpu.make_async_copy(src, dst, w_sem.at[k])

    load(0, w_qkv.at[0], wq_v).start()
    kv_copy = pltpu.make_async_copy(kv_ref, cache, kv_sem)
    kv_copy.start()
    load(1, w_o.at[0], wo_v).start()
    load(2, w_up.at[0], wu_v).start()
    load(3, w_down.at[0], wd_v).start()
    pl.semaphore_wait(barrier, len(ORDER) + 4)

    def mod_copy(d):
        return pltpu.make_async_remote_copy(src_ref=mod_ref, dst_ref=mods.at[me], send_sem=m_send.at[d], recv_sem=m_recv.at[d], device_id=peer_of(d)[1], device_id_type=MESH)

    for d in ORDER:
        mod_copy(d).start()
    mods[me] = mod_ref[...]
    for d in ORDER:
        mod_copy(d).wait()

    lane = lax.broadcasted_iota(jnp.int32, (rows, 128), 1)
    low = lane < head_dim
    scale = head_dim ** -0.5 * math.log2(math.e)
    tdims = (((1,), (1,)), ((), ()))

    def qkv_copy(d, slot):
        peer, place = peer_of(d)
        return pltpu.make_async_remote_copy(src_ref=send.at[peer], dst_ref=recv.at[slot, me], send_sem=q_send.at[d], recv_sem=q_recv.at[slot, d], device_id=place, device_id_type=MESH)

    def own_copy(slot):
        return pltpu.make_async_copy(send.at[me], recv.at[slot, me], q_recv.at[slot, 0])

    def o_copy(g):
        return pltpu.make_async_remote_copy(src_ref=obuf.at[g], dst_ref=back.at[me], send_sem=o_send.at[g], recv_sem=o_recv.at[me], device_id=place_of(g), device_id_type=MESH)

    def own_back(g):
        return pltpu.make_async_copy(obuf.at[g], back.at[g], o_recv.at[g])

    def window(col):
        t, off = col // 128, col % 128
        if off == 0:
            return qkv[:, t * 128:t * 128 + 128]
        if off + head_dim <= 128:
            return pltpu.roll(qkv[:, t * 128:t * 128 + 128], 128 - off, 1)
        return pltpu.roll(qkv[:, t * 128:t * 128 + 256], 256 - off, 1)[:, :128]

    def layer_body(it, carry):
        layer = it % layers
        step = it // layers
        slot = it % 2
        nxt = (it + 1) % layers
        more = it + 1 < 2 * layers

        def mod(which, j):
            return mods[2 * layer + which, pl.ds(step * 3 + j, 1), :]

        @pl.when(layer == 0)
        def _():
            emb = jnp.dot(xbuf[...].astype(bf16), w_in_ref[...], preferred_element_type=f32) + pos_ref[...].astype(f32)
            hid[...] = emb.astype(bf16)

        normed = (layer_norm(hid[...].astype(f32)) * (1.0 + mod(0, 0)) + mod(0, 1)).astype(bf16)
        load(0, w_qkv.at[layer], wq_v).wait()

        def qkv_body(j, c):
            cols = pl.ds(pl.multiple_of(j * width, 128), width)
            qkv[:, cols] = jnp.dot(normed, wq_v[:, cols], preferred_element_type=f32) + bias_ref[layer, :, cols]
            return c
        lax.fori_loop(0, 3, qkv_body, 0)

        @pl.when(more)
        def _():
            load(0, w_qkv.at[nxt], wq_v).start()

        for g in range(GROUP):
            q, k, v = (window(part * width + g * head_dim) for part in range(3))
            send[g, :, :128] = jnp.where(low, q, pltpu.roll(v, head_dim, 1)).astype(bf16)
            send[g, :, 128:] = jnp.where(low, k, pltpu.roll(v, 2 * head_dim - 128, 1)).astype(bf16)
        for d in ORDER:
            qkv_copy(d, slot).start()
        own_copy(slot).start()

        @pl.when(it == 0)
        def _():
            kv_copy.wait()

        for d in ORDER:
            qkv_copy(d, slot).wait()
        own_copy(slot).wait()

        half = GROUP // 2
        for b in range(half):
            query = recv[slot, 2 * b:2 * b + 2, :, :128].reshape(2 * rows, 128)
            query = jnp.where(jnp.concatenate([low, low], axis=0), query.astype(f32), 0.0).astype(bf16)
            blk0 = recv[slot, :half].reshape(half * rows, 256)
            if b < half // 2:
                blk1 = cache[layer]
            else:
                blk1 = recv[slot, half:].reshape(half * rows, 256)
            log0 = lax.dot_general(query, blk0[:, 128:], tdims, preferred_element_type=f32)
            log1 = lax.dot_general(query, blk1[:, 128:], tdims, preferred_element_type=f32)
            peak = jnp.maximum(jnp.max(log0, axis=-1, keepdims=True), jnp.max(log1, axis=-1, keepdims=True))
            exp0 = jnp.exp2((log0 - peak) * scale)
            exp1 = jnp.exp2((log1 - peak) * scale)
            inv = 1.0 / (jnp.sum(exp0, axis=-1, keepdims=True) + jnp.sum(exp1, axis=-1, keepdims=True))
            out = jnp.dot((exp0 * inv).astype(bf16), blk0, preferred_element_type=f32) + jnp.dot((exp1 * inv).astype(bf16), blk1, preferred_element_type=f32)
            low2 = lax.broadcasted_iota(jnp.int32, (2 * rows, 128), 1) >= head_dim
            both = jnp.where(low2, out[:, :128], pltpu.roll(out[:, 128:], 128 - head_dim, 1))
            both = pltpu.roll(both, 128 - head_dim, 1).astype(bf16)
            obuf[2 * b:2 * b + 2] = both.reshape(2, rows, 128)
            for g in (2 * b, 2 * b + 1):
                @pl.when(me != g)
                def _():
                    o_copy(g).start()

                @pl.when(me == g)
                def _():
                    own_back(g).start()
        cache[layer] = recv[slot, half:].reshape(half * rows, 256)

        for g in range(GROUP):
            own_back(g).wait()
            attn[:, g * head_dim:(g + 1) * head_dim] = back[g, :, :head_dim]

        load(1, w_o.at[layer], wo_v).wait()
        proj = jnp.dot(attn[...], wo_v[...], preferred_element_type=f32) + bias_ref[layer, :, 3 * width:4 * width]
        res = hid[...].astype(f32) + mod(0, 2) * proj
        resid[...] = res

        @pl.when(more)
        def _():
            load(1, w_o.at[nxt], wo_v).start()

        mlp_in = (layer_norm(res) * (1.0 + mod(1, 0)) + mod(1, 1)).astype(bf16)
        load(2, w_up.at[layer], wu_v).wait()

        def up_body(j, c):
            cols = pl.ds(pl.multiple_of(j * width, 128), width)
            bcols = pl.ds(pl.multiple_of((j + 4) * width, 128), width)
            up = jnp.dot(mlp_in, wu_v[:, cols], preferred_element_type=f32) + bias_ref[layer, :, bcols]
            mid[j] = jax.nn.gelu(up, approximate=True).astype(bf16)
            return c
        lax.fori_loop(0, 4, up_body, 0)

        @pl.when(more)
        def _():
            load(2, w_up.at[nxt], wu_v).start()

        load(3, w_down.at[layer], wd_v).wait()

        def down_body(j, acc):
            return acc + jnp.dot(mid[j], wd_v[pl.ds(pl.multiple_of(j * width, 128), width), :], preferred_element_type=f32)
        down = lax.fori_loop(0, 4, down_body, jnp.zeros((rows, width), f32))
        hidden = (resid[...] + mod(1, 2) * (down + bias_ref[layer, :, 8 * width:9 * width])).astype(bf16)
        hid[...] = hidden

        @pl.when(more)
        def _():
            load(3, w_down.at[nxt], wd_v).start()

        for g in range(GROUP):
            @pl.when(me != g)
            def _():
                o_copy(g).wait_send()

        @pl.when(layer == layers - 1)
        def _():
            out_in = (layer_norm(hidden.astype(f32)) * (1.0 + fin_ref[step, 0:1, :]) + fin_ref[step, 1:2, :]).astype(bf16)
            vel = jnp.dot(out_in, w_out_ref[...], preferred_element_type=f32)
            xbuf[...] = xbuf[...] + step_ref[step] * vel
        return carry

    xbuf[...] = latent_ref[...]
    lax.fori_loop(0, 2 * layers, layer_body, 0)

    def x_copy(k):
        return pltpu.make_async_remote_copy(src_ref=xbuf, dst_ref=xall.at[dp * 2 + zc], send_sem=x_send.at[k], recv_sem=x_recv.at[dp * 2 + zc], device_id=(image, k, sp), device_id_type=MESH)

    own = pltpu.make_async_copy(xbuf, xall.at[dp * 2 + zc], x_recv.at[dp * 2 + zc])
    for k in range(4):
        mine = jnp.logical_and(image == dp, pp == k)

        @pl.when(jnp.logical_not(mine))
        def _():
            x_copy(k).start()

        @pl.when(mine)
        def _():
            own.start()
    for k in range(4):
        pltpu.make_async_copy(xbuf, xall.at[k], x_recv.at[k]).wait()
        mine = jnp.logical_and(image == dp, pp == k)

        @pl.when(jnp.logical_not(mine))
        def _():
            x_copy(k).wait_send()
    out_ref[...] = xall[...]


def solution(mesh):
    row_spec = P("dp", "sp", None)
    full_spec = P()
    buf_spec = P("dp", None, None, None)
    in_specs = (row_spec, P(None, "sp", None), P("dp", None), P("dp"), full_spec, full_spec, full_spec, full_spec, full_spec, full_spec, full_spec, full_spec, full_spec, full_spec, buf_spec, buf_spec)

    def device_fn(latent_in, pos_embed, condition, step_size, w_in, w_ada, w_qkv, w_o, w_up, w_down, b_layer, w_fa, b_fa, w_out, k_old, v_old):
        f32, bf16 = jnp.float32, jnp.bfloat16
        num_patches, sub_rows, patch_dim = latent_in.shape
        width = w_in.shape[1]
        layers = w_qkv.shape[0]
        head_dim = k_old.shape[3]
        patch_rows = k_old.shape[1] // num_patches
        rows = sub_rows // 2
        dp, pp, sp = lax.axis_index("dp"), lax.axis_index("pp"), lax.axis_index("sp")
        zc, image = pp % 2, pp // 2
        me = dp * 8 + zc * 4 + sp
        local = image == dp
        swap = [(0, 1), (1, 0)]

        def heads_of(buf, head):
            return lax.dynamic_slice(buf, (0, patch_rows, head, 0), (layers, patch_rows, 1, head_dim)).reshape(layers, patch_rows * head_dim // 128, 128)

        def rows_of(patch):
            return lax.dynamic_slice(latent_in, (patch, zc * rows, 0), (1, rows, patch_dim)).reshape(-1)

        other = (1 - dp) * 8 + zc * 4 + sp
        kv_send = jnp.concatenate([heads_of(k_old, other), heads_of(v_old, other)], axis=0)
        kv_got = lax.ppermute(kv_send, "dp", swap)
        kv_own = jnp.concatenate([heads_of(k_old, me), heads_of(v_old, me)], axis=0)
        small = jnp.concatenate([condition.astype(f32).reshape(-1), step_size])
        pack_got = lax.ppermute(jnp.concatenate([rows_of(1 - dp), small]), "dp", swap)
        pack = jnp.where(local, jnp.concatenate([rows_of(dp), small]), pack_got)
        latent = pack[:rows * patch_dim].reshape(rows, patch_dim)
        cond32 = pack[rows * patch_dim:rows * patch_dim + 2 * width].reshape(2, width)
        steps = jnp.broadcast_to(pack[-2:].reshape(2, 1, 1), (2, 1, patch_dim))
        pos = lax.dynamic_slice(pos_embed, (dp, zc * rows, 0), (1, rows, width))[0]

        cond = jax.nn.silu(cond32).astype(bf16)
        piece = 3 * width
        w_mine = lax.dynamic_slice(w_ada, (me // 2, 0, (me % 2) * piece), (1, width, piece))[0]
        b_mine = lax.dynamic_slice(b_layer, (me // 2, (me % 2) * piece), (1, piece)).astype(f32)
        mod_mine = (jnp.dot(cond, w_mine, preferred_element_type=f32) + b_mine).reshape(6, width)
        fin = (jnp.dot(cond, w_fa, preferred_element_type=f32) + b_fa.astype(f32)).reshape(2, 2, width)
        bias = b_layer[:, 6 * width:].astype(f32).reshape(layers, 1, 9 * width)

        kv = jnp.where(local, kv_own, kv_got).reshape(2, layers, patch_rows, head_dim)
        head_gap = 128 - head_dim
        kept = jnp.concatenate([jnp.zeros_like(kv[0]), kv[1, ..., :head_gap], kv[0], kv[1, ..., head_gap:], jnp.zeros((layers, patch_rows, 256 - 3 * head_dim), bf16)], axis=-1)

        vmem = pl.BlockSpec(memory_space=pltpu.VMEM)
        hbm = pl.BlockSpec(memory_space=pl.ANY)
        dma = pltpu.SemaphoreType.DMA
        out = pl.pallas_call(
            functools.partial(step_kernel, (rows, width, layers, head_dim)),
            out_shape=jax.ShapeDtypeStruct((4, rows, patch_dim), f32),
            in_specs=[vmem] * 8 + [hbm] * 5,
            out_specs=vmem,
            scratch_shapes=[
                pltpu.VMEM((width, 3 * width), bf16),
                pltpu.VMEM((width, width), bf16),
                pltpu.VMEM((width, 4 * width), bf16),
                pltpu.VMEM((4 * width, width), bf16),
                pltpu.VMEM((GROUP, 6, width), f32),
                pltpu.VMEM((layers, patch_rows, 256), bf16),
                pltpu.VMEM((GROUP, rows, 256), bf16),
                pltpu.VMEM((2, GROUP, rows, 256), bf16),
                pltpu.VMEM((GROUP, rows, 128), bf16),
                pltpu.VMEM((GROUP, rows, 128), bf16),
                pltpu.VMEM((rows, 3 * width), f32),
                pltpu.VMEM((rows, width), bf16),
                pltpu.VMEM((4, rows, width), bf16),
                pltpu.VMEM((rows, width), bf16),
                pltpu.VMEM((rows, width), f32),
                pltpu.VMEM((rows, patch_dim), f32),
                pltpu.VMEM((4, rows, patch_dim), f32),
                dma((4,)), dma, dma((GROUP,)), dma((GROUP,)), dma((GROUP,)), dma((2, GROUP)), dma((GROUP,)), dma((GROUP,)), dma((4,)), dma((4,)),
            ],
            compiler_params=pltpu.CompilerParams(collective_id=0, has_side_effects=True, vmem_limit_bytes=60 * 1024 * 1024),
        )(latent, pos, steps, w_in, w_out, mod_mine, fin, bias, kept, w_qkv, w_o, w_up, w_down)
        return out.reshape(num_patches, sub_rows, patch_dim)

    return jax.shard_map(device_fn, mesh=mesh, in_specs=in_specs, out_specs=row_spec, check_vma=False)
```

time: 1010 us -> 540 us (0.53)
  Pallas kernels: 99.3 us -> 468 us
  matrix products: 274 us -> 7.76 us
  waiting for transfers between devices: 254 us -> 15.8 us
  blocking collectives: 179 us -> 0 us
  starting transfers between devices: 85.1 us -> 3.07 us
  local copies, waits for them, and re-layouts: 96.9 us -> 40.9 us
    pallas_call x16 -> x1, Pallas kernels: 99.3 us -> 468 us  [device_fn(): pl.pallas_call(functools.partial(step_kernel, (rows, width, layers, head_...]
    dot_general x54 -> x2, matrix products: 274 us -> 7.76 us  [the longest x1 4.46 us: device_fn(): jnp.dot(cond, w_mine, preferred_element_type=f32) + b_mine]
    all_to_all x22 -> x0, waiting for transfers between devices: 254 us -> none  [the longest x16 202 us: device_fn(): lax.all_to_all(send, axes, split_axis=0, concat_axis=0, tiled=True)]
    all_to_all x10 -> x0, blocking collectives: 142 us -> none  [device_fn(): lax.all_to_all(out.reshape(group, rows, head_dim), axes, split_axis=0, co...]
    all_to_all x22 -> x0, starting transfers between devices: 85.1 us -> none  [the longest x16 58.8 us: device_fn(): lax.all_to_all(send, axes, split_axis=0, concat_axis=0, tiled=True)]
    reshape x68 -> x14, local copies, waits for them, and re-layouts: 55.6 us -> 17.1 us  [the longest x4 8.56 us: heads_of(): lax.dynamic_slice(buf, (0, patch_rows, head, 0), (layers, patch_rows, 1,...]
    all_gather x2 -> x0, blocking collectives: 37.4 us -> none  [the longest x1 24.3 us: device_fn(): mod_all = lax.all_gather(mod_mine, axes, axis=0, tiled=False)]
    unnamed x272 -> x21, local copies, waits for them, and re-layouts: 25.4 us -> 0.94 us
  transfers between devices with their start and end apart: 22 -> 2, of which waited for: 22 -> 1; matrix products, arithmetic and copies ran while one was open for 3% -> 4% of each run, Pallas kernels for 0% -> 0%
where the time goes in v2:
time: 540 us
  Pallas kernels  468 us (87%)
  local copies, waits for them, and re-layouts  40.9 us (8%)
  waiting for transfers between devices  15.8 us (3%)
  matrix products  7.76 us (1%)
    pallas_call x1, Pallas kernels, device_fn(): pl.pallas_call(functools.partial(step_kernel, (rows, width, layers, head_...  468 us
    ppermute x1, waiting for transfers between devices, device_fn(): lax.ppermute(jnp.concatenate([rows_of(1 - dp), small]), 'dp', swap)  15.8 us
  transfers between devices with their start and end apart: 2, of which 1 were waited for; matrix products, arithmetic and copies ran while one was open for 4% of the time, Pallas kernels for 0%

profile of v2, /device:TPU:0, one launch (start us, length us, event | category | flops | bytes accessed | tf_op | source)
XLA Modules:
  0.0 539.6 jit_solution(17026501468586893165)
XLA Ops:
  0.0 2.7 constant_dynamic-slice_fusion.2
  2.7 1.6 copy.23
  4.3 2.6 reshape.73
  7.5 1.7 reshape.74
  9.3 2.2 pad_maximum_fusion
  11.5 3.0 collective-permute-start.1
  14.8 0.9 slice_convert_fusion
  17.1 1.7 reshape.71
  19.5 2.6 reshape.72
  22.2 1.0 reshape.81.bias_ref
  23.2 0.9 copy.25.w_out_ref
  24.1 0.9 convert_reduce_fusion
  25.0 15.8 %collective-permute-done = f32[3330]{0:T(1024)S(1)} collective-permute-done((f32[3330]{0:T(1024)S(1)}, f32[3330]{0:T(1024)S(1)}, u32[]{:S(2)}, u32[]{:S(2)}) %collective-permute-start) | collective-permute-done | bytes 13352 | tf_op jit(solution)/shard_map/ppermute | solution.py:278
  40.9 4.5 fusion.3
  46.0 3.3 convolution_add_fusion
  50.8 3.9 reshape.75
  54.7 1.4 slice_bitcast_fusion
  56.0 1.0 slice_bitcast_fusion.1
  58.0 3.0 squeeze.18
  61.0 1.1 broadcast_in_dim.13
  62.1 1.1 broadcast_in_dim.14
  63.2 6.5 %concatenate.22.kv_ref = bf16[8,512,256]{2,1,0:T(8,128)(2,1)} concatenate(bf16[8,512,72]{2,1,0:T(8,128)(2,1)} %broadcast_in_dim.13, bf16[8,512,56]{2,1,0:T(8,128)(2,1)S(1)} %copy-done.3, bf16[8,512,72]{2,1,0:T(8,128)(2,1)S(1)} %squeeze.18, bf16[8,512,16]{2,1,0:T(8,128)(2,1)S(1)} %copy-done.2, bf16[8,512,40]{2,1,0:T(8,128)(2,1)} %broadcast_in_dim.14), dimensions={2} | concatenate | bytes 4194304 | tf_op jit(solution)/shard_map/concatenate | solution.py:295
  70.4 467.7 %shard_map.154 = f32[4,64,16]{2,1,0:T(8,128)} custom-call(f32[64,16]{1,0:T(8,128)} %reshape.65.latent_ref, bf16[64,1152]{1,0:T(8,128)(2,1)} %dynamic-slice_bitcast_fusion.pos_ref, f32[2,1,16]{2,1,0:T(1,128)} %broadcast_in_dim.12.step_ref, bf16[16,1152]{1,0:T(8,128)(2,1)} %w_in_ref.1, bf16[1152,16]{1,0:T(8,128)(2,1)} %copy.25.w_out_ref, ...), custom_call_target="tpu_custom_call" | custom-call | tf_op jit(solution)/shard_map/pallas_call | solution.py:300
  538.0 1.6 copy.26
  (46 shorter events, 6.8 us)
Async XLA Ops:
  0.0 15.8 %copy-start = (bf16[2,128,1152]{2,1,0:T(8,128)(2,1)S(1)}, bf16[2,128,1152]{2,1,0:T(8,128)(2,1)}, u32[]{:S(2)}) copy-start(bf16[2,128,1152]{2,1,0:T(8,128)(2,1)} %param.17) | copy-start | bytes 1769476
  2.7 11.8 %copy-start.6 = (f32[2,128,16]{1,2,0:T(8,128)S(1)}, f32[2,128,16]{1,2,0:T(8,128)}, u32[]{:S(2)}) copy-start(f32[2,128,16]{1,2,0:T(8,128)} %param.16) | copy-start | bytes 49156
  2.7 12.0 %copy-start.8 = (bf16[2,1152]{1,0:T(2,128)(2,1)S(1)}, bf16[2,1152]{1,0:T(2,128)(2,1)}, u32[]{:S(2)}) copy-start(bf16[2,1152]{1,0:T(2,128)(2,1)} %param.18) | copy-start | bytes 13828
  2.7 12.0 %copy-start.9 = (f32[2]{0:T(128)S(1)}, f32[2]{0:T(128)}, u32[]{:S(2)}) copy-start(f32[2]{0:T(128)} %param.19) | copy-start | bytes 28
  9.2 13.0 %copy-start.7 = (bf16[2304]{0:T(1024)(128)(2,1)S(1)}, bf16[2304]{0:T(1024)(128)(2,1)}, u32[]{:S(2)}) copy-start(bf16[2304]{0:T(1024)(128)(2,1)} %param.28) | copy-start | bytes 13828
  9.3 13.9 %copy-start.5 = (bf16[1152,16]{0,1:T(8,128)(2,1)S(1)}, bf16[1152,16]{0,1:T(8,128)(2,1)}, u32[]{:S(2)}) copy-start(bf16[1152,16]{0,1:T(8,128)(2,1)} %param.29) | copy-start | bytes 110596
  11.5 39.1 %collective-permute-start.1 = (bf16[16,288,128]{2,1,0:T(8,128)(2,1)}, bf16[16,288,128]{2,1,0:T(8,128)(2,1)}, u32[]{:S(2)}, u32[]{:S(2)}) collective-permute-start(bf16[16,288,128]{2,1,0:T(8,128)(2,1)} %pad_maximum_fusion), channel_id=1, source_target_pairs={{0,16},{16,0},{1,17},{17,1},{2,18},{18,2},{3,19},{19,3},{4,20},{20... | collective-permute-start | bytes 3538952 | tf_op jit(solution)/shard_map/ppermute | solution.py:275
  14.8 26.0 %collective-permute-start = (f32[3330]{0:T(1024)S(1)}, f32[3330]{0:T(1024)S(1)}, u32[]{:S(2)}, u32[]{:S(2)}) collective-permute-start(f32[3330]{0:T(1024)S(1)} %pad_maximum_fusion.1), channel_id=1, source_target_pairs={{0,16},{16,0},{1,17},{17,1},{2,18},{18,2},{3,19},{19,3},{4,20},{20... | collective-permute-start | bytes 39968 | tf_op jit(solution)/shard_map/ppermute | solution.py:278
  40.9 9.8 %copy-start.4 = (bf16[8,288,128]{2,1,0:T(8,128)(2,1)S(1)}, bf16[8,288,128]{2,1,0:T(8,128)(2,1)}, u32[]{:S(2)}) copy-start(bf16[8,288,128]{2,1,0:T(8,128)(2,1)} %reshape.72) | copy-start | bytes 1769476
  57.1 6.1 %copy-start.2 = (bf16[8,512,16]{2,1,0:T(8,128)(2,1)S(1)}, bf16[8,512,16]{2,1,0:T(8,128)(2,1)}, u32[]{:S(2)}) copy-start(bf16[8,512,16]{2,1,0:T(8,128)(2,1)} %slice_bitcast_fusion) | copy-start | bytes 393220
  57.1 6.1 %copy-start.3 = (bf16[8,512,56]{2,1,0:T(8,128)(2,1)S(1)}, bf16[8,512,56]{2,1,0:T(8,128)(2,1)}, u32[]{:S(2)}) copy-start(bf16[8,512,56]{2,1,0:T(8,128)(2,1)} %slice_bitcast_fusion.1) | copy-start | bytes 1376260
  70.4 469.3 %copy-start.1 = (bf16[2,128,1152]{2,1,0:T(8,128)(2,1)S(1)}, bf16[2,128,1152]{2,1,0:T(8,128)(2,1)}, u32[]{:S(2)}) copy-start(bf16[2,128,1152]{2,1,0:T(8,128)(2,1)} %param.17) | copy-start | bytes 1769476

commit v3 on v2

v3 whole, which is shorter than its diff:
```python
import functools
import math

import jax
import jax.numpy as jnp
from jax import lax
from jax.experimental import pallas as pl
from jax.experimental.pallas import tpu as pltpu
from jax.sharding import PartitionSpec as P

LN_EPS = 1e-6
GROUP = 16
MESH = pl.DeviceIdType.MESH
ORDER = (15, 7, 14, 6, 13, 5, 12, 4, 11, 3, 10, 2, 9, 8, 1)


def layer_norm(hidden):
    mean_val = jnp.mean(hidden, axis=-1, keepdims=True)
    centered = hidden - mean_val
    var_val = jnp.mean(centered * centered, axis=-1, keepdims=True)
    return centered * lax.rsqrt(var_val + LN_EPS)


def step_kernel(dims, latent_ref, pos_ref, step_ref, w_in_ref, w_out_ref, mod_ref, fin_ref, bias_ref, k_pair, v_pair, w_qkv, w_o, w_up, w_down, out_ref,
                wq_v, wo_v, wu_v, wd_v, mods, cache, k_raw, v_raw, send, recv, obuf, back, qkv, attn, mid, hid, resid, xbuf, xall,
                w_sem, k_sem, v_sem, k_send, v_send, m_send, m_recv, q_send, q_recv, o_send, o_recv, x_send, x_recv):
    rows, width, layers, head_dim = dims
    bf16, f32 = jnp.bfloat16, jnp.float32
    dp, pp, sp = lax.axis_index("dp"), lax.axis_index("pp"), lax.axis_index("sp")
    zc, yc, cc = pp % 2, sp // 2, sp % 2
    image = pp // 2
    me = dp * 8 + zc * 4 + sp
    local = image == dp
    total = 2 * layers

    def peer_of(d):
        x, z, y, c = (dp + d // 8) % 2, (zc + (d // 4) % 2) % 2, (yc + (d // 2) % 2) % 2, (cc + d % 2) % 2
        s = y * 2 + c
        return x * 8 + z * 4 + s, (x, image * 2 + z, s)

    def place_of(g):
        return (g // 8, image * 2 + (g // 4) % 2, g % 4)

    barrier = pltpu.get_barrier_semaphore()
    for d in ORDER:
        pl.semaphore_signal(barrier, inc=1, device_id=peer_of(d)[1], device_id_type=MESH)
    for k in range(4):
        pl.semaphore_signal(barrier, inc=1, device_id=(k // 2, (1 - image) * 2 + k % 2, sp), device_id_type=MESH)

    def load(k, src, dst):
        return pltpu.make_async_copy(src, dst, w_sem.at[k])

    load(0, w_qkv.at[0], wq_v).start()
    load(1, w_o.at[0], wo_v).start()
    load(2, w_up.at[0], wu_v).start()
    load(3, w_down.at[0], wd_v).start()
    pl.semaphore_wait(barrier, len(ORDER) + 4)

    def mod_copy(d):
        return pltpu.make_async_remote_copy(src_ref=mod_ref, dst_ref=mods.at[me], send_sem=m_send.at[d], recv_sem=m_recv.at[d], device_id=peer_of(d)[1], device_id_type=MESH)

    for d in ORDER:
        mod_copy(d).start()
    mods[me] = mod_ref[...]

    def old_copies(layer):
        return (pltpu.make_async_copy(k_pair.at[dp, layer], k_raw.at[layer], k_sem.at[layer]),
                pltpu.make_async_copy(v_pair.at[dp, layer], v_raw.at[layer], v_sem.at[layer]))

    def old_sends(layer):
        there = (1 - dp, pp, sp)
        return (pltpu.make_async_remote_copy(src_ref=k_pair.at[1 - dp, layer], dst_ref=k_raw.at[layer], send_sem=k_send.at[layer], recv_sem=k_sem.at[layer], device_id=there, device_id_type=MESH),
                pltpu.make_async_remote_copy(src_ref=v_pair.at[1 - dp, layer], dst_ref=v_raw.at[layer], send_sem=v_send.at[layer], recv_sem=v_sem.at[layer], device_id=there, device_id_type=MESH))

    def old_start(layer):
        @pl.when(local)
        def _():
            for copy in old_sends(layer) + old_copies(layer):
                copy.start()

    old_start(0)
    for d in ORDER:
        mod_copy(d).wait()

    lane = lax.broadcasted_iota(jnp.int32, (rows, 128), 1)
    low = lane < head_dim
    scale = head_dim ** -0.5 * math.log2(math.e)
    tdims = (((1,), (1,)), ((), ()))

    def qkv_copy(p, d, slot):
        peer, place = peer_of(d)
        return pltpu.make_async_remote_copy(src_ref=send.at[p, peer], dst_ref=recv.at[p, slot, me], send_sem=q_send.at[p, d], recv_sem=q_recv.at[p, slot, d], device_id=place, device_id_type=MESH)

    def own_copy(p, slot):
        return pltpu.make_async_copy(send.at[p, me], recv.at[p, slot, me], q_recv.at[p, slot, 0])

    def o_copy(p, g):
        return pltpu.make_async_remote_copy(src_ref=obuf.at[p, g], dst_ref=back.at[p, me], send_sem=o_send.at[p, g], recv_sem=o_recv.at[p, me], device_id=place_of(g), device_id_type=MESH)

    def own_back(p, g):
        return pltpu.make_async_copy(obuf.at[p, g], back.at[p, g], o_recv.at[p, g])

    def window(col):
        t, off = col // 128, col % 128
        if off == 0:
            return qkv[:, t * 128:t * 128 + 128]
        if off + head_dim <= 128:
            return pltpu.roll(qkv[:, t * 128:t * 128 + 128], 128 - off, 1)
        return pltpu.roll(qkv[:, t * 128:t * 128 + 256], 256 - off, 1)[:, :128]

    def finish(p, it):
        layer = (it + layers - 1) % layers
        step = (it - 1) // layers
        nxt = it % layers
        refill = jnp.logical_and(p == 1, it < total)

        def mod(which, j):
            return mods[2 * layer + which, pl.ds(step * 3 + j, 1), :]

        for g in range(GROUP):
            own_back(p, g).wait()
            attn[:, g * head_dim:(g + 1) * head_dim] = back[p, g, :, :head_dim]
        if p == 0:
            load(1, w_o.at[layer], wo_v).wait()
        proj = jnp.dot(attn[...], wo_v[...], preferred_element_type=f32) + bias_ref[layer, :, 3 * width:4 * width]
        res = hid[p].astype(f32) + mod(0, 2) * proj
        resid[...] = res
        mlp_in = (layer_norm(res) * (1.0 + mod(1, 0)) + mod(1, 1)).astype(bf16)

        @pl.when(refill)
        def _():
            load(1, w_o.at[nxt], wo_v).start()

        if p == 0:
            load(2, w_up.at[layer], wu_v).wait()

        def up_body(j, c):
            cols = pl.ds(pl.multiple_of(j * width, 128), width)
            bcols = pl.ds(pl.multiple_of((j + 4) * width, 128), width)
            up = jnp.dot(mlp_in, wu_v[:, cols], preferred_element_type=f32) + bias_ref[layer, :, bcols]
            mid[j] = jax.nn.gelu(up, approximate=True).astype(bf16)
            return c
        lax.fori_loop(0, 4, up_body, 0)

        @pl.when(refill)
        def _():
            load(2, w_up.at[nxt], wu_v).start()

        if p == 0:
            load(3, w_down.at[layer], wd_v).wait()
        down = jnp.dot(jnp.concatenate([mid[j] for j in range(4)], axis=1), wd_v[...], preferred_element_type=f32)
        hidden = (resid[...] + mod(1, 2) * (down + bias_ref[layer, :, 8 * width:9 * width])).astype(bf16)
        hid[p] = hidden

        @pl.when(refill)
        def _():
            load(3, w_down.at[nxt], wd_v).start()

        for g in range(GROUP):
            @pl.when(me != g)
            def _():
                o_copy(p, g).wait_send()

        @pl.when(layer == layers - 1)
        def _():
            out_in = (layer_norm(hidden.astype(f32)) * (1.0 + fin_ref[step, 0:1, :]) + fin_ref[step, 1:2, :]).astype(bf16)
            vel = jnp.dot(out_in, w_out_ref[...], preferred_element_type=f32)
            xbuf[p] = xbuf[p] + step_ref[step] * vel

    def begin(p, it):
        layer = it % layers
        step = it // layers
        slot = it % 2

        def mod(which, j):
            return mods[2 * layer + which, pl.ds(step * 3 + j, 1), :]

        @pl.when(layer == 0)
        def _():
            emb = jnp.dot(xbuf[p].astype(bf16), w_in_ref[...], preferred_element_type=f32) + pos_ref[p].astype(f32)
            hid[p] = emb.astype(bf16)

        normed = (layer_norm(hid[p].astype(f32)) * (1.0 + mod(0, 0)) + mod(0, 1)).astype(bf16)
        if p == 0:
            load(0, w_qkv.at[layer], wq_v).wait()
        qkv[...] = jnp.dot(normed, wq_v[...], preferred_element_type=f32) + bias_ref[layer, :, :3 * width]

        if p == 1:
            @pl.when(it + 1 < total)
            def _():
                load(0, w_qkv.at[(it + 1) % layers], wq_v).start()

        for g in range(GROUP):
            q, k, v = (window(part * width + g * head_dim) for part in range(3))
            send[p, g, :, :128] = jnp.where(low, q, pltpu.roll(v, head_dim, 1)).astype(bf16)
            send[p, g, :, 128:] = jnp.where(low, k, pltpu.roll(v, 2 * head_dim - 128, 1)).astype(bf16)
        for d in ORDER:
            qkv_copy(p, d, slot).start()
        own_copy(p, slot).start()

    def attend(p, it):
        layer = it % layers
        slot = it % 2
        for d in ORDER:
            qkv_copy(p, d, slot).wait()
        own_copy(p, slot).wait()
        per = GROUP // 4
        wide = per * rows
        for fx, fz in ((1, 1), (1, 0), (0, 1), (0, 0)):
            block = (dp + fx) % 2 * 2 + (zc + fz) % 2
            query = recv[p, slot, pl.ds(block * per, per), :, :128].reshape(wide, 128)
            wide_lane = lax.broadcasted_iota(jnp.int32, (wide, 128), 1)
            query = jnp.where(wide_lane < head_dim, query.astype(f32), 0.0).astype(bf16)
            blk0 = recv[0, slot].reshape(GROUP * rows, 256)
            blk1 = cache[layer] if p == 0 else recv[1, slot].reshape(GROUP * rows, 256)
            log0 = lax.dot_general(query, blk0[:, 128:], tdims, preferred_element_type=f32)
            log1 = lax.dot_general(query, blk1[:, 128:], tdims, preferred_element_type=f32)
            peak = jnp.maximum(jnp.max(log0, axis=-1, keepdims=True), jnp.max(log1, axis=-1, keepdims=True))
            exp0 = jnp.exp2((log0 - peak) * scale)
            exp1 = jnp.exp2((log1 - peak) * scale)
            inv = 1.0 / (jnp.sum(exp0, axis=-1, keepdims=True) + jnp.sum(exp1, axis=-1, keepdims=True))
            out = jnp.dot((exp0 * inv).astype(bf16), blk0, preferred_element_type=f32) + jnp.dot((exp1 * inv).astype(bf16), blk1, preferred_element_type=f32)
            both = jnp.where(wide_lane >= head_dim, out[:, :128], pltpu.roll(out[:, 128:], 128 - head_dim, 1))
            both = pltpu.roll(both, 128 - head_dim, 1).astype(bf16)
            obuf[p, pl.ds(block * per, per)] = both.reshape(per, rows, 128)
            for i in range(per):
                g = block * per + i

                @pl.when(me != g)
                def _():
                    o_copy(p, g).start()

                @pl.when(me == g)
                def _():
                    own_back(p, g).start()

    def loop_body(it, carry):
        @pl.when(it < layers - 1)
        def _():
            old_start(it + 1)

        for p in range(2):
            @pl.when(it > 0)
            def _():
                finish(p, it)

            @pl.when(it < total)
            def _():
                begin(p, it)

        @pl.when(it < layers)
        def _():
            for copy in old_copies(it):
                copy.wait()
            for copy in old_sends(it):
                @pl.when(local)
                def _():
                    copy.wait_send()
            val = v_raw[it].astype(f32)
            old_lane = lax.broadcasted_iota(jnp.int32, val.shape, 1)
            cache[it, :, :128] = pltpu.roll(val, head_dim, 1).astype(bf16)
            cache[it, :, 128:] = jnp.where(old_lane < head_dim, k_raw[it].astype(f32), pltpu.roll(val, 2 * head_dim - 128, 1)).astype(bf16)

        @pl.when(it < total)
        def _():
            attend(0, it)
            attend(1, it)
            cache[it % layers] = recv[1, it % 2].reshape(GROUP * rows, 256)
        return carry

    xbuf[...] = latent_ref[...]
    lax.fori_loop(0, total + 1, loop_body, 0)

    def x_copy(k):
        return pltpu.make_async_remote_copy(src_ref=xbuf, dst_ref=xall.at[dp * 2 + zc], send_sem=x_send.at[k], recv_sem=x_recv.at[dp * 2 + zc], device_id=(image, k, sp), device_id_type=MESH)

    own = pltpu.make_async_copy(xbuf, xall.at[dp * 2 + zc], x_recv.at[dp * 2 + zc])
    for k in range(4):
        mine = jnp.logical_and(local, pp == k)

        @pl.when(jnp.logical_not(mine))
        def _():
            x_copy(k).start()

        @pl.when(mine)
        def _():
            own.start()
    for k in range(4):
        pltpu.make_async_copy(xbuf, xall.at[k], x_recv.at[k]).wait()
        mine = jnp.logical_and(local, pp == k)

        @pl.when(jnp.logical_not(mine))
        def _():
            x_copy(k).wait_send()
    for p in range(2):
        for k in range(4):
            out_ref[p, k * rows:(k + 1) * rows, :] = xall[k, p]


def solution(mesh):
    row_spec = P("dp", "sp", None)
    full_spec = P()
    buf_spec = P("dp", None, None, None)
    in_specs = (row_spec, P(None, "sp", None), P("dp", None), P("dp"), full_spec, full_spec, full_spec, full_spec, full_spec, full_spec, full_spec, full_spec, full_spec, full_spec, buf_spec, buf_spec)

    def device_fn(latent_in, pos_embed, condition, step_size, w_in, w_ada, w_qkv, w_o, w_up, w_down, b_layer, w_fa, b_fa, w_out, k_old, v_old):
        f32, bf16 = jnp.float32, jnp.bfloat16
        num_patches, sub_rows, patch_dim = latent_in.shape
        width = w_in.shape[1]
        layers = w_qkv.shape[0]
        head_dim = k_old.shape[3]
        patch_rows = k_old.shape[1] // num_patches
        rows = sub_rows // 4
        dp, pp, sp = lax.axis_index("dp"), lax.axis_index("pp"), lax.axis_index("sp")
        zc, image = pp % 2, pp // 2
        me = dp * 8 + zc * 4 + sp
        local = image == dp
        swap = [(0, 1), (1, 0)]

        def rows_of(quarter):
            return lax.dynamic_slice(latent_in, (0, quarter * rows, 0), (num_patches, rows, patch_dim)).reshape(-1)

        count = num_patches * rows * patch_dim
        small = jnp.concatenate([condition.astype(f32).reshape(-1), step_size])
        pack_got = lax.ppermute(jnp.concatenate([rows_of((1 - dp) * 2 + zc), small]), "dp", swap)
        pack = jnp.where(local, jnp.concatenate([rows_of(dp * 2 + zc), small]), pack_got)
        latent = pack[:count].reshape(num_patches, rows, patch_dim)
        cond32 = pack[count:count + 2 * width].reshape(2, width)
        steps = jnp.broadcast_to(pack[-2:].reshape(2, 1, 1), (2, 1, patch_dim))
        pos = lax.dynamic_slice(pos_embed, (0, (dp * 2 + zc) * rows, 0), (num_patches, rows, width))

        cond = jax.nn.silu(cond32).astype(bf16)
        piece = 3 * width
        w_mine = lax.dynamic_slice(w_ada, (me // 2, 0, (me % 2) * piece), (1, width, piece))[0]
        b_mine = lax.dynamic_slice(b_layer, (me // 2, (me % 2) * piece), (1, piece)).astype(f32)
        mod_mine = (jnp.dot(cond, w_mine, preferred_element_type=f32) + b_mine).reshape(6, width)
        fin = (jnp.dot(cond, w_fa, preferred_element_type=f32) + b_fa.astype(f32)).reshape(2, 2, width)
        bias = b_layer[:, 6 * width:].astype(f32).reshape(layers, 1, 9 * width)

        def heads_of(buf, head):
            part = lax.dynamic_slice(buf, (0, patch_rows, head, 0), (layers, patch_rows, 1, head_dim)).reshape(layers, patch_rows, head_dim)
            return jnp.pad(part, ((0, 0), (0, 0), (0, 128 - head_dim)))

        head = zc * 4 + sp
        k_pair = jnp.stack([heads_of(k_old, head), heads_of(k_old, head + 8)])
        v_pair = jnp.stack([heads_of(v_old, head), heads_of(v_old, head + 8)])

        vmem = pl.BlockSpec(memory_space=pltpu.VMEM)
        hbm = pl.BlockSpec(memory_space=pl.ANY)
        dma = pltpu.SemaphoreType.DMA
        return pl.pallas_call(
            functools.partial(step_kernel, (rows, width, layers, head_dim)),
            out_shape=jax.ShapeDtypeStruct((num_patches, sub_rows, patch_dim), f32),
            in_specs=[vmem] * 8 + [hbm] * 6,
            out_specs=vmem,
            scratch_shapes=[
                pltpu.VMEM((width, 3 * width), bf16),
                pltpu.VMEM((width, width), bf16),
                pltpu.VMEM((width, 4 * width), bf16),
                pltpu.VMEM((4 * width, width), bf16),
                pltpu.VMEM((GROUP, 6, width), f32),
                pltpu.VMEM((layers, patch_rows, 256), bf16),
                pltpu.VMEM((layers, patch_rows, 128), bf16),
                pltpu.VMEM((layers, patch_rows, 128), bf16),
                pltpu.VMEM((2, GROUP, rows, 256), bf16),
                pltpu.VMEM((2, 2, GROUP, rows, 256), bf16),
                pltpu.VMEM((2, GROUP, rows, 128), bf16),
                pltpu.VMEM((2, GROUP, rows, 128), bf16),
                pltpu.VMEM((rows, 3 * width), f32),
                pltpu.VMEM((rows, width), bf16),
                pltpu.VMEM((4, rows, width), bf16),
                pltpu.VMEM((2, rows, width), bf16),
                pltpu.VMEM((rows, width), f32),
                pltpu.VMEM((2, rows, patch_dim), f32),
                pltpu.VMEM((4, 2, rows, patch_dim), f32),
                dma((4,)), dma((layers,)), dma((layers,)), dma((layers,)), dma((layers,)), dma((GROUP,)), dma((GROUP,)), dma((2, GROUP)), dma((2, 2, GROUP)),
                dma((2, GROUP)), dma((2, GROUP)), dma((4,)), dma((4,)),
            ],
            compiler_params=pltpu.CompilerParams(collective_id=0, has_side_effects=True, vmem_limit_bytes=60 * 1024 * 1024),
        )(latent, pos, steps, w_in, w_out, mod_mine, fin, bias, k_pair, v_pair, w_qkv, w_o, w_up, w_down)

    return jax.shard_map(device_fn, mesh=mesh, in_specs=in_specs, out_specs=row_spec, check_vma=False)
```

time: 540 us -> 468 us (0.87)
  Pallas kernels: 468 us -> 429 us
  local copies, waits for them, and re-layouts: 40.9 us -> 19.2 us
  waiting for transfers between devices: 15.8 us -> 0.01 us
    pallas_call x1, Pallas kernels: 468 us -> 429 us  [device_fn(): pl.pallas_call(functools.partial(step_kernel, (rows, width, layers, head_...]
    ppermute x2 -> x1, waiting for transfers between devices: 15.8 us -> 0.01 us  [device_fn(): lax.ppermute(jnp.concatenate([rows_of((1 - dp) * 2 + zc), small]), 'dp',...]
    reshape x10 -> x4, local copies, waits for them, and re-layouts: 14.9 us -> 0.84 us  [the longest x1 0.67 us: device_fn(): latent = pack[:count].reshape(num_patches, rows, patch_dim)]
    concatenate x1 -> x0, local copies, waits for them, and re-layouts: 6.5 us -> none  [device_fn(): jnp.concatenate([jnp.zeros_like(kv[0]), kv[1, ..., :head_gap], kv[0], kv[...]
    squeeze x4 -> x0, local copies, waits for them, and re-layouts: 6.1 us -> none  [the longest x1 2.99 us: device_fn(): kv[0]]
    another operation x0 -> x2, other arithmetic: none -> 5.49 us  [the longest x1 2.76 us: device_fn(): v_pair = jnp.stack([heads_of(v_old, head), heads_of(v_old, head + 8)])]
  transfers between devices with their start and end apart: 2 -> 1, of which waited for: 1 -> 0; matrix products, arithmetic and copies ran while one was open for 4% -> 4% of each run, Pallas kernels for 0% -> 0%
where the time goes in v3:
time: 468 us; the launch traced here: 466 us
  Pallas kernels  429 us (92%)
  local copies, waits for them, and re-layouts  19.2 us (4%)
  matrix products  7.7 us (2%)
  other arithmetic  7.58 us (2%)
    pallas_call x1, Pallas kernels, device_fn(): pl.pallas_call(functools.partial(step_kernel, (rows, width, layers, head_...  429 us
  transfers between devices with their start and end apart: 1, of which 0 were waited for; matrix products, arithmetic and copies ran while one was open for 4% of the time, Pallas kernels for 0%

profile of v3, /device:TPU:0, one launch (start us, length us, event | category | flops | bytes accessed | tf_op | source)
XLA Modules:
  0.0 466.3 jit_solution(9486200692646488348)
XLA Ops:
  0.0 1.5 constant_dynamic-slice_fusion.6
  1.6 0.7 reshape.68
  2.3 1.3 pad_maximum_fusion.2
  3.6 3.0 collective-permute-start
  6.6 2.9 constant_dynamic-slice_fusion.1
  9.5 0.6 copy.28
  10.4 1.5 copy.27
  11.9 1.2 pad_bitcast_fusion.1
  13.1 1.5 copy.26
  14.6 1.2 pad_bitcast_fusion.2
  15.8 0.6 copy.25
  16.7 0.7 constant_dynamic-slice_fusion.4.pos_ref
  17.4 2.8 pad_maximum_fusion.1.v_pair
  20.2 2.7 pad_maximum_fusion.k_pair
  23.1 0.9 reshape.71.bias_ref
  24.0 0.9 copy.29.w_out_ref
  25.1 0.7 fusion.6
  25.8 4.4 fusion.3
  30.2 0.7 reshape.58.mod_ref
  30.9 3.3 convolution_add_fusion
  34.2 0.6 reshape.60.fin_ref
  34.8 0.7 reshape.57.latent_ref
  36.1 428.6 %shard_map.154 = f32[2,128,16]{2,1,0:T(8,128)} custom-call(f32[2,32,16]{2,1,0:T(8,128)} %reshape.57.latent_ref, bf16[2,32,1152]{2,1,0:T(8,128)(2,1)} %constant_dynamic-slice_fusion.4.pos_ref, f32[2,1,16]{2,1,0:T(1,128)} %broadcast_in_dim.2.step_ref, bf16[16,1152]{1,0:T(8,128)(2,1)} %w_in_ref.1, bf16[1152,16]{1,0:T(8,128)(2,1)} %copy.29.w_out_ref, ...), custom_call_target="tpu_custom_call" | custom-call | tf_op jit(solution)/shard_map/pallas_call | solution.py:351
  464.7 1.6 copy.30
  (32 shorter events, 1.6 us)
Async XLA Ops:
  0.0 16.7 %copy-start = (bf16[2,128,1152]{2,1,0:T(8,128)(2,1)S(1)}, bf16[2,128,1152]{2,1,0:T(8,128)(2,1)}, u32[]{:S(2)}) copy-start(bf16[2,128,1152]{2,1,0:T(8,128)(2,1)} %param.17) | copy-start | bytes 1769476
  2.3 4.3 copy-start.3
  3.6 21.4 %collective-permute-start = (f32[3330]{0:T(1024)}, f32[3330]{0:T(1024)}, u32[]{:S(2)}, u32[]{:S(2)}) collective-permute-start(f32[3330]{0:T(1024)} %pad_maximum_fusion.2), channel_id=1, source_target_pairs={{0,16},{16,0},{1,17},{17,1},{2,18},{18,2},{3,19},{19,3},{4,20},{20... | collective-permute-start | bytes 39968 | tf_op jit(solution)/shard_map/ppermute | solution.py:325
  9.5 7.9 %copy-start.2 = (bf16[8,17280]{1,0:T(8,128)(2,1)S(1)}, bf16[8,17280]{1,0:T(8,128)(2,1)}, u32[]{:S(2)}) copy-start(bf16[8,17280]{1,0:T(8,128)(2,1)} %param.26) | copy-start | bytes 829444
  16.4 6.5 %copy-start.5 = (f32[2,32,16]{1,2,0:T(8,128)S(1)}, f32[2,32,16]{1,2,0:T(8,128)}, u32[]{:S(2)}) copy-start(f32[2,32,16]{1,2,0:T(8,128)} %get-tuple-element.11) | copy-start | bytes 12292
  16.5 6.6 %copy-start.7 = (bf16[2304]{0:T(1024)(128)(2,1)S(1)}, bf16[2304]{0:T(1024)(128)(2,1)}, u32[]{:S(2)}) copy-start(bf16[2304]{0:T(1024)(128)(2,1)} %param.28) | copy-start | bytes 13828
  16.5 7.6 %copy-start.6 = (bf16[1152,16]{0,1:T(8,128)(2,1)S(1)}, bf16[1152,16]{0,1:T(8,128)(2,1)}, u32[]{:S(2)}) copy-start(bf16[1152,16]{0,1:T(8,128)(2,1)} %param.29) | copy-start | bytes 110596
  16.5 8.6 %copy-start.4 = (f32[2304]{0:T(1024)S(1)}, f32[2304]{0:T(1024)}, u32[]{:S(2)}) copy-start(f32[2304]{0:T(1024)} %copy-done.3) | copy-start | bytes 27652
  36.1 430.2 %copy-start.1 = (bf16[2,128,1152]{2,1,0:T(8,128)(2,1)S(1)}, bf16[2,128,1152]{2,1,0:T(8,128)(2,1)}, u32[]{:S(2)}) copy-start(bf16[2,128,1152]{2,1,0:T(8,128)(2,1)} %param.17) | copy-start | bytes 1769476

commit v4 on v3

--- a/solution.py
+++ b/solution.py
@@ -12,6 +12,7 @@
 GROUP = 16
 MESH = pl.DeviceIdType.MESH
 ORDER = (15, 7, 14, 6, 13, 5, 12, 4, 11, 3, 10, 2, 9, 8, 1)
+CHIPS = (7, 3, 6, 2, 5, 1, 4)
 
 
 def layer_norm(hidden):
@@ -21,9 +22,9 @@
     return centered * lax.rsqrt(var_val + LN_EPS)
 
 
-def step_kernel(dims, latent_ref, pos_ref, step_ref, w_in_ref, w_out_ref, mod_ref, fin_ref, bias_ref, k_pair, v_pair, w_qkv, w_o, w_up, w_down, out_ref,
-                wq_v, wo_v, wu_v, wd_v, mods, cache, k_raw, v_raw, send, recv, obuf, back, qkv, attn, mid, hid, resid, xbuf, xall,
-                w_sem, k_sem, v_sem, k_send, v_send, m_send, m_recv, q_send, q_recv, o_send, o_recv, x_send, x_recv):
+def step_kernel(dims, latent_ref, pos_ref, step_ref, w_in_ref, w_out_ref, mod_ref, fin_ref, bias_ref, k_mine, v_mine, k_other, v_other, w_qkv, w_o, w_up, w_down, out_ref,
+                wq_v, wo_v, wu_v, wd_v, mods, cache, k_raw, v_raw, pack, recv, obuf, back, qkv, attn, mid, hid, resid, xbuf, xall,
+                w_sem, k_sem, v_sem, k_send, v_send, m_send, m_recv, q_send, q_recv, o_send, o_recv, d_send, d_recv, e_send, e_recv, x_send, x_recv):
     rows, width, layers, head_dim = dims
     bf16, f32 = jnp.bfloat16, jnp.float32
     dp, pp, sp = lax.axis_index("dp"), lax.axis_index("pp"), lax.axis_index("sp")
@@ -38,8 +39,12 @@
         s = y * 2 + c
         return x * 8 + z * 4 + s, (x, image * 2 + z, s)
 
-    def place_of(g):
-        return (g // 8, image * 2 + (g // 4) % 2, g % 4)
+    chip = dp * 4 + zc * 2 + yc
+    partner = (dp, pp, yc * 2 + (1 - cc))
+
+    def chip_of(d):
+        x, z, y = (dp + d // 4) % 2, (zc + (d // 2) % 2) % 2, (yc + d % 2) % 2
+        return x * 4 + z * 2 + y, (x, image * 2 + z, y * 2 + cc)
 
     barrier = pltpu.get_barrier_semaphore()
     for d in ORDER:
@@ -64,13 +69,13 @@
     mods[me] = mod_ref[...]
 
     def old_copies(layer):
-        return (pltpu.make_async_copy(k_pair.at[dp, layer], k_raw.at[layer], k_sem.at[layer]),
-                pltpu.make_async_copy(v_pair.at[dp, layer], v_raw.at[layer], v_sem.at[layer]))
+        return (pltpu.make_async_copy(k_mine.at[layer], k_raw.at[layer], k_sem.at[layer]),
+                pltpu.make_async_copy(v_mine.at[layer], v_raw.at[layer], v_sem.at[layer]))
 
     def old_sends(layer):
         there = (1 - dp, pp, sp)
-        return (pltpu.make_async_remote_copy(src_ref=k_pair.at[1 - dp, layer], dst_ref=k_raw.at[layer], send_sem=k_send.at[layer], recv_sem=k_sem.at[layer], device_id=there, device_id_type=MESH),
-                pltpu.make_async_remote_copy(src_ref=v_pair.at[1 - dp, layer], dst_ref=v_raw.at[layer], send_sem=v_send.at[layer], recv_sem=v_sem.at[layer], device_id=there, device_id_type=MESH))
+        return (pltpu.make_async_remote_copy(src_ref=k_other.at[layer], dst_ref=k_raw.at[layer], send_sem=k_send.at[layer], recv_sem=k_sem.at[layer], device_id=there, device_id_type=MESH),
+                pltpu.make_async_remote_copy(src_ref=v_other.at[layer], dst_ref=v_raw.at[layer], send_sem=v_send.at[layer], recv_sem=v_sem.at[layer], device_id=there, device_id_type=MESH))
 
     def old_start(layer):
         @pl.when(local)
@@ -87,18 +92,33 @@
     scale = head_dim ** -0.5 * math.log2(math.e)
     tdims = (((1,), (1,)), ((), ()))
 
+    both = pl.ds(0, 2)
+
+    def qkv_swap(p):
+        return pltpu.make_async_remote_copy(src_ref=pack.at[p, 2], dst_ref=pack.at[p, 1], send_sem=d_send.at[p], recv_sem=d_recv.at[p], device_id=partner, device_id_type=MESH)
+
     def qkv_copy(p, d, slot):
-        peer, place = peer_of(d)
-        return pltpu.make_async_remote_copy(src_ref=send.at[p, peer], dst_ref=recv.at[p, slot, me], send_sem=q_send.at[p, d], recv_sem=q_recv.at[p, slot, d], device_id=place, device_id_type=MESH)
-
-    def own_copy(p, slot):
-        return pltpu.make_async_copy(send.at[p, me], recv.at[p, slot, me], q_recv.at[p, slot, 0])
-
-    def o_copy(p, g):
-        return pltpu.make_async_remote_copy(src_ref=obuf.at[p, g], dst_ref=back.at[p, me], send_sem=o_send.at[p, g], recv_sem=o_recv.at[p, me], device_id=place_of(g), device_id_type=MESH)
-
-    def own_back(p, g):
-        return pltpu.make_async_copy(obuf.at[p, g], back.at[p, g], o_recv.at[p, g])
+        there, place = chip_of(d)
+        return pltpu.make_async_remote_copy(src_ref=pack.at[p, both, there], dst_ref=recv.at[p, slot, both, chip], send_sem=q_send.at[p, d], recv_sem=q_recv.at[p, slot, d], device_id=place, device_id_type=MESH)
+
+    def o_copy(p, d):
+        there, place = chip_of(d)
+        return pltpu.make_async_remote_copy(src_ref=obuf.at[p, both, there], dst_ref=back.at[p, both, chip], send_sem=o_send.at[p, d], recv_sem=o_recv.at[p, d], device_id=place, device_id_type=MESH)
+
+    def o_swap(p):
+        return pltpu.make_async_remote_copy(src_ref=back.at[p, 1], dst_ref=back.at[p, 2], send_sem=e_send.at[p], recv_sem=e_recv.at[p], device_id=partner, device_id_type=MESH)
+
+    def spread(p, it):
+        slot = it % 2
+        qkv_swap(p).wait()
+        for d in CHIPS:
+            qkv_copy(p, d, slot).start()
+        recv[p, slot, :, chip] = pack[p, both, chip]
+
+    def relay(p):
+        for d in CHIPS:
+            o_copy(p, d).wait()
+        o_swap(p).start()
 
     def window(col):
         t, off = col // 128, col % 128
@@ -117,14 +137,18 @@
         def mod(which, j):
             return mods[2 * layer + which, pl.ds(step * 3 + j, 1), :]
 
+        o_swap(p).wait()
         for g in range(GROUP):
-            own_back(p, g).wait()
-            attn[:, g * head_dim:(g + 1) * head_dim] = back[p, g, :, :head_dim]
+            attn[:, g * head_dim:(g + 1) * head_dim] = back[p, (g + cc) % 2 * 2, g // 2, :, :head_dim]
         if p == 0:
             load(1, w_o.at[layer], wo_v).wait()
         proj = jnp.dot(attn[...], wo_v[...], preferred_element_type=f32) + bias_ref[layer, :, 3 * width:4 * width]
         res = hid[p].astype(f32) + mod(0, 2) * proj
         resid[...] = res
+        if p == 1:
+            @pl.when(it < total)
+            def _():
+                spread(0, it)
         mlp_in = (layer_norm(res) * (1.0 + mod(1, 0)) + mod(1, 1)).astype(bf16)
 
         @pl.when(refill)
@@ -156,10 +180,8 @@
         def _():
             load(3, w_down.at[nxt], wd_v).start()
 
-        for g in range(GROUP):
-            @pl.when(me != g)
-            def _():
-                o_copy(p, g).wait_send()
+        if p == 0:
+            relay(1)
 
         @pl.when(layer == layers - 1)
         def _():
@@ -192,23 +214,20 @@
 
         for g in range(GROUP):
             q, k, v = (window(part * width + g * head_dim) for part in range(3))
-            send[p, g, :, :128] = jnp.where(low, q, pltpu.roll(v, head_dim, 1)).astype(bf16)
-            send[p, g, :, 128:] = jnp.where(low, k, pltpu.roll(v, 2 * head_dim - 128, 1)).astype(bf16)
-        for d in ORDER:
-            qkv_copy(p, d, slot).start()
-        own_copy(p, slot).start()
+            place = (g + cc) % 2 * 2
+            pack[p, place, g // 2, :, :128] = jnp.where(low, q, pltpu.roll(v, head_dim, 1)).astype(bf16)
+            pack[p, place, g // 2, :, 128:] = jnp.where(low, k, pltpu.roll(v, 2 * head_dim - 128, 1)).astype(bf16)
+        qkv_swap(p).start()
 
     def attend(p, it):
         layer = it % layers
         slot = it % 2
-        for d in ORDER:
+        for d in CHIPS:
             qkv_copy(p, d, slot).wait()
-        own_copy(p, slot).wait()
-        per = GROUP // 4
-        wide = per * rows
+        wide = 4 * rows
         for fx, fz in ((1, 1), (1, 0), (0, 1), (0, 0)):
             block = (dp + fx) % 2 * 2 + (zc + fz) % 2
-            query = recv[p, slot, pl.ds(block * per, per), :, :128].reshape(wide, 128)
+            query = recv[p, slot, :, pl.ds(block * 2, 2), :, :128].reshape(wide, 128)
             wide_lane = lax.broadcasted_iota(jnp.int32, (wide, 128), 1)
             query = jnp.where(wide_lane < head_dim, query.astype(f32), 0.0).astype(bf16)
             blk0 = recv[0, slot].reshape(GROUP * rows, 256)
@@ -220,29 +239,33 @@
             exp1 = jnp.exp2((log1 - peak) * scale)
             inv = 1.0 / (jnp.sum(exp0, axis=-1, keepdims=True) + jnp.sum(exp1, axis=-1, keepdims=True))
             out = jnp.dot((exp0 * inv).astype(bf16), blk0, preferred_element_type=f32) + jnp.dot((exp1 * inv).astype(bf16), blk1, preferred_element_type=f32)
-            both = jnp.where(wide_lane >= head_dim, out[:, :128], pltpu.roll(out[:, 128:], 128 - head_dim, 1))
-            both = pltpu.roll(both, 128 - head_dim, 1).astype(bf16)
-            obuf[p, pl.ds(block * per, per)] = both.reshape(per, rows, 128)
-            for i in range(per):
-                g = block * per + i
-
-                @pl.when(me != g)
-                def _():
-                    o_copy(p, g).start()
-
-                @pl.when(me == g)
-                def _():
-                    own_back(p, g).start()
+            rolled = jnp.where(wide_lane >= head_dim, out[:, :128], pltpu.roll(out[:, 128:], 128 - head_dim, 1))
+            obuf[p, :, pl.ds(block * 2, 2)] = pltpu.roll(rolled, 128 - head_dim, 1).astype(bf16).reshape(2, 2, rows, 128)
+            for fy in (1, 0):
+                d = fx * 4 + fz * 2 + fy
+                if d:
+                    o_copy(p, d).start()
+                else:
+                    back[p, both, chip] = obuf[p, :, chip]
 
     def loop_body(it, carry):
         @pl.when(it < layers - 1)
         def _():
             old_start(it + 1)
+
+        @pl.when(it > 0)
+        def _():
+            relay(0)
 
         for p in range(2):
             @pl.when(it > 0)
             def _():
                 finish(p, it)
+
+            if p == 1:
+                @pl.when(it == 0)
+                def _():
+                    spread(0, it)
 
             @pl.when(it < total)
             def _():
@@ -256,13 +279,14 @@
                 @pl.when(local)
                 def _():
                     copy.wait_send()
-            val = v_raw[it].astype(f32)
-            old_lane = lax.broadcasted_iota(jnp.int32, val.shape, 1)
-            cache[it, :, :128] = pltpu.roll(val, head_dim, 1).astype(bf16)
-            cache[it, :, 128:] = jnp.where(old_lane < head_dim, k_raw[it].astype(f32), pltpu.roll(val, 2 * head_dim - 128, 1)).astype(bf16)
+            gap = 128 - head_dim
+            val = v_raw[it]
+            cache[it, :, :128] = jnp.concatenate([jnp.zeros_like(val), val[:, :gap]], axis=1)
+            cache[it, :, 128:] = jnp.concatenate([k_raw[it], val[:, gap:], jnp.zeros((val.shape[0], 256 - 3 * head_dim), bf16)], axis=1)
 
         @pl.when(it < total)
         def _():
+            spread(1, it)
             attend(0, it)
             attend(1, it)
             cache[it % layers] = recv[1, it % 2].reshape(GROUP * rows, 256)
@@ -338,12 +362,10 @@
         bias = b_layer[:, 6 * width:].astype(f32).reshape(layers, 1, 9 * width)
 
         def heads_of(buf, head):
-            part = lax.dynamic_slice(buf, (0, patch_rows, head, 0), (layers, patch_rows, 1, head_dim)).reshape(layers, patch_rows, head_dim)
-            return jnp.pad(part, ((0, 0), (0, 0), (0, 128 - head_dim)))
-
-        head = zc * 4 + sp
-        k_pair = jnp.stack([heads_of(k_old, head), heads_of(k_old, head + 8)])
-        v_pair = jnp.stack([heads_of(v_old, head), heads_of(v_old, head + 8)])
+            return lax.dynamic_slice(buf, (0, patch_rows, head, 0), (layers, patch_rows, 1, head_dim)).reshape(layers, patch_rows, head_dim)
+
+        other = (1 - dp) * 8 + zc * 4 + sp
+        olds = [heads_of(k_old, me), heads_of(v_old, me), heads_of(k_old, other), heads_of(v_old, other)]
 
         vmem = pl.BlockSpec(memory_space=pltpu.VMEM)
         hbm = pl.BlockSpec(memory_space=pl.ANY)
@@ -351,7 +373,7 @@
         return pl.pallas_call(
             functools.partial(step_kernel, (rows, width, layers, head_dim)),
             out_shape=jax.ShapeDtypeStruct((num_patches, sub_rows, patch_dim), f32),
-            in_specs=[vmem] * 8 + [hbm] * 6,
+            in_specs=[vmem] * 8 + [hbm] * 8,
             out_specs=vmem,
             scratch_shapes=[
                 pltpu.VMEM((width, 3 * width), bf16),
@@ -360,12 +382,12 @@
                 pltpu.VMEM((4 * width, width), bf16),
                 pltpu.VMEM((GROUP, 6, width), f32),
                 pltpu.VMEM((layers, patch_rows, 256), bf16),
-                pltpu.VMEM((layers, patch_rows, 128), bf16),
-                pltpu.VMEM((layers, patch_rows, 128), bf16),
-                pltpu.VMEM((2, GROUP, rows, 256), bf16),
-                pltpu.VMEM((2, 2, GROUP, rows, 256), bf16),
-                pltpu.VMEM((2, GROUP, rows, 128), bf16),
-                pltpu.VMEM((2, GROUP, rows, 128), bf16),
+                pltpu.VMEM((layers, patch_rows, head_dim), bf16),
+                pltpu.VMEM((layers, patch_rows, head_dim), bf16),
+                pltpu.VMEM((2, 3, 8, rows, 256), bf16),
+                pltpu.VMEM((2, 2, 2, 8, rows, 256), bf16),
+                pltpu.VMEM((2, 2, 8, rows, 128), bf16),
+                pltpu.VMEM((2, 3, 8, rows, 128), bf16),
                 pltpu.VMEM((rows, 3 * width), f32),
                 pltpu.VMEM((rows, width), bf16),
                 pltpu.VMEM((4, rows, width), bf16),
@@ -373,10 +395,10 @@
                 pltpu.VMEM((rows, width), f32),
                 pltpu.VMEM((2, rows, patch_dim), f32),
                 pltpu.VMEM((4, 2, rows, patch_dim), f32),
-                dma((4,)), dma((layers,)), dma((layers,)), dma((layers,)), dma((layers,)), dma((GROUP,)), dma((GROUP,)), dma((2, GROUP)), dma((2, 2, GROUP)),
-                dma((2, GROUP)), dma((2, GROUP)), dma((4,)), dma((4,)),
+                dma((4,)), dma((layers,)), dma((layers,)), dma((layers,)), dma((layers,)), dma((GROUP,)), dma((GROUP,)), dma((2, 8)), dma((2, 2, 8)),
+                dma((2, 8)), dma((2, 8)), dma((2,)), dma((2,)), dma((2,)), dma((2,)), dma((4,)), dma((4,)),
             ],
             compiler_params=pltpu.CompilerParams(collective_id=0, has_side_effects=True, vmem_limit_bytes=60 * 1024 * 1024),
-        )(latent, pos, steps, w_in, w_out, mod_mine, fin, bias, k_pair, v_pair, w_qkv, w_o, w_up, w_down)
+        )(latent, pos, steps, w_in, w_out, mod_mine, fin, bias, *olds, w_qkv, w_o, w_up, w_down)
 
     return jax.shard_map(device_fn, mesh=mesh, in_specs=in_specs, out_specs=row_spec, check_vma=False)

time: 468 us -> 470 us (level)
  Pallas kernels: 429 us -> 436 us
    pallas_call x1, Pallas kernels: 429 us -> 436 us  [device_fn(): pl.pallas_call(functools.partial(step_kernel, (rows, width, layers, head_...]
    another operation x2 -> x0, other arithmetic: 5.49 us -> none  [the longest x1 2.76 us: device_fn(): v_pair = jnp.stack([heads_of(v_old, head), heads_of(v_old, head + 8)])]
  transfers between devices with their start and end apart: 1 -> 1, of which waited for: 0 -> 0; matrix products, arithmetic and copies ran while one was open for 4% -> 3% of each run, Pallas kernels for 0% -> 0%
where the time goes in v4:
time: 470 us; the launch traced here: 467 us
  Pallas kernels  436 us (93%)
  local copies, waits for them, and re-layouts  16.3 us (3%)
  matrix products  7.7 us (2%)
    pallas_call x1, Pallas kernels, device_fn(): pl.pallas_call(functools.partial(step_kernel, (rows, width, layers, head_...  436 us
  transfers between devices with their start and end apart: 1, of which 0 were waited for; matrix products, arithmetic and copies ran while one was open for 3% of the time, Pallas kernels for 0%

profile of v4, /device:TPU:0, one launch (start us, length us, event | category | flops | bytes accessed | tf_op | source)
XLA Modules:
  0.0 466.7 jit_solution(6712413200568692613)
XLA Ops:
  0.0 0.9 constant_dynamic-slice_fusion.6
  1.0 0.7 reshape.68
  1.7 0.7 pad_maximum_fusion
  2.4 3.0 collective-permute-start
  5.4 0.7 constant_dynamic-slice_fusion.4.pos_ref
  6.1 0.9 slice_convert_fusion
  7.0 1.8 constant_dynamic-slice_fusion
  8.9 1.3 copy.25
  10.1 1.3 copy.26
  11.4 1.3 copy.27
  12.7 1.3 copy.28
  14.2 0.7 convert_element_type.23
  14.9 0.9 reshape.71.bias_ref
  15.8 1.7 copy.29.w_out_ref
  17.5 0.9 convert_reduce_fusion
  18.4 0.7 fusion.6
  19.1 4.4 fusion.3
  23.5 0.7 reshape.58.mod_ref
  24.2 3.3 convolution_add_fusion
  27.5 0.7 reshape.60.fin_ref
  28.2 0.7 reshape.57.latent_ref
  28.8 0.6 broadcast_in_dim.2.step_ref
  29.5 435.6 %shard_map.154 = f32[2,128,16]{2,1,0:T(8,128)} custom-call(f32[2,32,16]{2,1,0:T(8,128)} %reshape.57.latent_ref, bf16[2,32,1152]{2,1,0:T(8,128)(2,1)} %constant_dynamic-slice_fusion.4.pos_ref, f32[2,1,16]{2,1,0:T(1,128)} %broadcast_in_dim.2.step_ref, bf16[16,1152]{1,0:T(8,128)(2,1)} %w_in_ref.1, bf16[1152,16]{1,0:T(8,128)(2,1)} %copy.29.w_out_ref, ...), custom_call_target="tpu_custom_call" | custom-call | tf_op jit(solution)/shard_map/pallas_call | solution.py:373
  465.1 1.6 copy.30
  (14 shorter events, 0.4 us)
Async XLA Ops:
  0.0 5.4 %copy-start = (bf16[2,128,1152]{2,1,0:T(8,128)(2,1)S(1)}, bf16[2,128,1152]{2,1,0:T(8,128)(2,1)}, u32[]{:S(2)}) copy-start(bf16[2,128,1152]{2,1,0:T(8,128)(2,1)} %param.17) | copy-start | bytes 1769476
  2.4 16.0 %collective-permute-start = (f32[3330]{0:T(1024)S(1)}, f32[3330]{0:T(1024)S(1)}, u32[]{:S(2)}, u32[]{:S(2)}) collective-permute-start(f32[3330]{0:T(1024)S(1)} %pad_maximum_fusion), channel_id=1, source_target_pairs={{0,16},{16,0},{1,17},{17,1},{2,18},{18,2},{3,19},{19,3},{4,20},{20... | collective-permute-start | bytes 39968 | tf_op jit(solution)/shard_map/ppermute | solution.py:349
  29.5 437.2 %copy-start.1 = (bf16[2,128,1152]{2,1,0:T(8,128)(2,1)S(1)}, bf16[2,128,1152]{2,1,0:T(8,128)(2,1)}, u32[]{:S(2)}) copy-start(bf16[2,128,1152]{2,1,0:T(8,128)(2,1)} %param.17) | copy-start | bytes 1769476

commit v5 on v4

--- a/solution.py
+++ b/solution.py
@@ -163,12 +163,12 @@
             bcols = pl.ds(pl.multiple_of((j + 4) * width, 128), width)
             up = jnp.dot(mlp_in, wu_v[:, cols], preferred_element_type=f32) + bias_ref[layer, :, bcols]
             mid[j] = jax.nn.gelu(up, approximate=True).astype(bf16)
+
+            @pl.when(refill)
+            def _():
+                load(2, w_up.at[nxt, :, cols], wu_v.at[:, cols]).start()
             return c
         lax.fori_loop(0, 4, up_body, 0)
-
-        @pl.when(refill)
-        def _():
-            load(2, w_up.at[nxt], wu_v).start()
 
         if p == 0:
             load(3, w_down.at[layer], wd_v).wait()
@@ -176,10 +176,6 @@
         hidden = (resid[...] + mod(1, 2) * (down + bias_ref[layer, :, 8 * width:9 * width])).astype(bf16)
         hid[p] = hidden
 
-        @pl.when(refill)
-        def _():
-            load(3, w_down.at[nxt], wd_v).start()
-
         if p == 0:
             relay(1)
 
@@ -206,11 +202,6 @@
         if p == 0:
             load(0, w_qkv.at[layer], wq_v).wait()
         qkv[...] = jnp.dot(normed, wq_v[...], preferred_element_type=f32) + bias_ref[layer, :, :3 * width]
-
-        if p == 1:
-            @pl.when(it + 1 < total)
-            def _():
-                load(0, w_qkv.at[(it + 1) % layers], wq_v).start()
 
         for g in range(GROUP):
             q, k, v = (window(part * width + g * head_dim) for part in range(3))
@@ -224,10 +215,16 @@
         slot = it % 2
         for d in CHIPS:
             qkv_copy(p, d, slot).wait()
-        wide = 4 * rows
-        for fx, fz in ((1, 1), (1, 0), (0, 1), (0, 0)):
-            block = (dp + fx) % 2 * 2 + (zc + fz) % 2
-            query = recv[p, slot, :, pl.ds(block * 2, 2), :, :128].reshape(wide, 128)
+        wide = 8 * rows
+        for fx in (1, 0):
+            first = (dp + fx) % 2 * 4
+            part = pl.ds((2 * p + 1 - fx) * width, width)
+
+            @pl.when(it > 0)
+            def _():
+                load(3, w_down.at[layer, part], wd_v.at[part]).start()
+
+            query = recv[p, slot, :, pl.ds(first, 4), :, :128].reshape(wide, 128)
             wide_lane = lax.broadcasted_iota(jnp.int32, (wide, 128), 1)
             query = jnp.where(wide_lane < head_dim, query.astype(f32), 0.0).astype(bf16)
             blk0 = recv[0, slot].reshape(GROUP * rows, 256)
@@ -240,9 +237,9 @@
             inv = 1.0 / (jnp.sum(exp0, axis=-1, keepdims=True) + jnp.sum(exp1, axis=-1, keepdims=True))
             out = jnp.dot((exp0 * inv).astype(bf16), blk0, preferred_element_type=f32) + jnp.dot((exp1 * inv).astype(bf16), blk1, preferred_element_type=f32)
             rolled = jnp.where(wide_lane >= head_dim, out[:, :128], pltpu.roll(out[:, 128:], 128 - head_dim, 1))
-            obuf[p, :, pl.ds(block * 2, 2)] = pltpu.roll(rolled, 128 - head_dim, 1).astype(bf16).reshape(2, 2, rows, 128)
-            for fy in (1, 0):
-                d = fx * 4 + fz * 2 + fy
+            obuf[p, :, pl.ds(first, 4)] = pltpu.roll(rolled, 128 - head_dim, 1).astype(bf16).reshape(2, 4, rows, 128)
+            for near in (3, 2, 1, 0):
+                d = fx * 4 + near
                 if d:
                     o_copy(p, d).start()
                 else:
@@ -289,6 +286,11 @@
             spread(1, it)
             attend(0, it)
             attend(1, it)
+
+            @pl.when(it + 1 < total)
+            def _():
+                load(0, w_qkv.at[(it + 1) % layers], wq_v).start()
+
             cache[it % layers] = recv[1, it % 2].reshape(GROUP * rows, 256)
         return carry
 

time: 470 us -> 450 us (0.957)
  Pallas kernels: 436 us -> 418 us
    pallas_call x1, Pallas kernels: 436 us -> 418 us  [device_fn(): pl.pallas_call(functools.partial(step_kernel, (rows, width, layers, head_...]
where the time goes in v5:
time: 450 us; the launch traced here: 449 us
  Pallas kernels  418 us (93%)
  local copies, waits for them, and re-layouts  16.3 us (4%)
  matrix products  7.7 us (2%)
    pallas_call x1, Pallas kernels, device_fn(): pl.pallas_call(functools.partial(step_kernel, (rows, width, layers, head_...  418 us
  transfers between devices with their start and end apart: 1, of which 0 were waited for; matrix products, arithmetic and copies ran while one was open for 3% of the time, Pallas kernels for 0%

profile of v5, /device:TPU:0, one launch (start us, length us, event | category | flops | bytes accessed | tf_op | source)
XLA Modules:
  0.0 449.1 jit_solution(212651724412399154)
XLA Ops:
  0.0 0.9 constant_dynamic-slice_fusion.6
  1.0 0.7 reshape.68
  1.7 0.7 pad_maximum_fusion
  2.4 3.0 collective-permute-start
  5.4 0.7 constant_dynamic-slice_fusion.4.pos_ref
  6.1 0.9 slice_convert_fusion
  7.0 1.8 constant_dynamic-slice_fusion
  8.9 1.3 copy.25
  10.1 1.3 copy.26
  11.4 1.3 copy.27
  12.7 1.3 copy.28
  14.2 0.7 convert_element_type.23
  14.9 0.9 reshape.71.bias_ref
  15.8 1.7 copy.29.w_out_ref
  17.5 0.9 convert_reduce_fusion
  18.4 0.7 fusion.6
  19.1 4.4 fusion.3
  23.5 0.7 reshape.58.mod_ref
  24.2 3.3 convolution_add_fusion
  27.5 0.7 reshape.60.fin_ref
  28.2 0.7 reshape.57.latent_ref
  28.8 0.6 broadcast_in_dim.2.step_ref
  29.5 418.1 %shard_map.154 = f32[2,128,16]{2,1,0:T(8,128)} custom-call(f32[2,32,16]{2,1,0:T(8,128)} %reshape.57.latent_ref, bf16[2,32,1152]{2,1,0:T(8,128)(2,1)} %constant_dynamic-slice_fusion.4.pos_ref, f32[2,1,16]{2,1,0:T(1,128)} %broadcast_in_dim.2.step_ref, bf16[16,1152]{1,0:T(8,128)(2,1)} %w_in_ref.1, bf16[1152,16]{1,0:T(8,128)(2,1)} %copy.29.w_out_ref, ...), custom_call_target="tpu_custom_call" | custom-call | tf_op jit(solution)/shard_map/pallas_call | solution.py:375
  447.5 1.6 copy.30
  (14 shorter events, 0.4 us)
Async XLA Ops:
  0.0 5.4 %copy-start = (bf16[2,128,1152]{2,1,0:T(8,128)(2,1)S(1)}, bf16[2,128,1152]{2,1,0:T(8,128)(2,1)}, u32[]{:S(2)}) copy-start(bf16[2,128,1152]{2,1,0:T(8,128)(2,1)} %param.17) | copy-start | bytes 1769476
  2.4 16.0 %collective-permute-start = (f32[3330]{0:T(1024)S(1)}, f32[3330]{0:T(1024)S(1)}, u32[]{:S(2)}, u32[]{:S(2)}) collective-permute-start(f32[3330]{0:T(1024)S(1)} %pad_maximum_fusion), channel_id=1, source_target_pairs={{0,16},{16,0},{1,17},{17,1},{2,18},{18,2},{3,19},{19,3},{4,20},{20... | collective-permute-start | bytes 39968 | tf_op jit(solution)/shard_map/ppermute | solution.py:351
  29.5 419.7 %copy-start.1 = (bf16[2,128,1152]{2,1,0:T(8,128)(2,1)S(1)}, bf16[2,128,1152]{2,1,0:T(8,128)(2,1)}, u32[]{:S(2)}) copy-start(bf16[2,128,1152]{2,1,0:T(8,128)(2,1)} %param.17) | copy-start | bytes 1769476
